TPU v7x, 32 devices: a whole 2x2x4 slice. The times are simulated.
32 devices in a mesh: dom: 8 (over y, x, core), sub: 4 (over z).
Axes of the slice: x: 2, y: 2, z: 4, core: 2. Of those that a mesh axis runs over, the one named last changes fastest.
Arguments:
- features: bfloat16 [32768, 602], P(('dom', 'sub')), may hold values from -6 to 6
- w_inner: bfloat16 [602, 256], replicated, may hold values from -0.25 to 0.25
- bias_inner: float32 [256], replicated, may hold values from -6 to 6
- w_outer: bfloat16 [256, 41], replicated, may hold values from -0.375 to 0.375
- bias_outer: float32 [41], replicated, may hold values from -6 to 6
- tiles: bfloat16 [256, 32, 128, 128], P(('dom', 'sub')), may hold values from -3 to 3
- tile_col: int32 [256, 32], P(('dom', 'sub')), may hold values from 0 to 39, as said below
- degrees: int32 [32768], P(('dom', 'sub')), may hold values from 1 to 32
- send_rows: int32 [32, 32, 128], P(('dom', 'sub')), may hold values from -1 to 1023, as said below
Outputs:
- logits: float32 [32768, 41], P(('dom', 'sub'))
Inputs may be any that keep to these rules, and one draw needn't show every extreme that they name: send_rows[e, p, s] is the row, among device e's 1024 vertices, that fills slot s of e's list for device p, or -1 for an unused slot; live slots come first and every list has 1 to 128 live slots; every sender has a full list, and in every draw some device receives full lists from all senders. tile_col[d * 8 + r, t] is the column block, in device d's column space, of tile t of row block r; the 32 column blocks of a row block are distinct.
All inputs are finite; a program needn't handle non-finite values.
Results may differ from a plain program's by a relative error of at most 0.0042.
Values may be sent and summed in bfloat16 or wider, within the bound.
No kernel may reach another device: no remote copies, remote signals or barrier semaphores. Data moves between devices by JAX's collectives and lax.ppermute only.
A program may use at most 128 MiB of HBM per device.

v0:
```python
import jax
import jax.numpy as jnp
from jax import lax
from jax.sharding import PartitionSpec as P


def deliver_inner(outgoing):
    return lax.all_to_all(outgoing, ("dom", "sub"), split_axis=0, concat_axis=0, tiled=True)


def deliver_outer(outgoing):
    return lax.all_to_all(outgoing, ("dom", "sub"), split_axis=0, concat_axis=0, tiled=True)


def aggregate(feature_rows, tiles, tile_col, send_lists, deliver):
    block_rows = tiles.shape[2]
    width = feature_rows.shape[1]
    clipped = jnp.clip(send_lists, 0, feature_rows.shape[0] - 1)
    live_slot = (send_lists >= 0)[:, :, None]
    outgoing = jnp.where(
        live_slot, jnp.take(feature_rows, clipped, axis=0), jnp.zeros((), feature_rows.dtype)
    )
    arrived = deliver(outgoing)
    columns = jnp.concatenate([feature_rows.reshape(-1, block_rows, width), arrived], axis=0)

    def rowblock(element):
        tile_set, col_set = element
        blocks = columns[col_set]
        return jnp.einsum("tij,tjw->iw", tile_set, blocks, preferred_element_type=jnp.float32)

    summed = lax.map(rowblock, (tiles, tile_col))
    return summed.reshape(feature_rows.shape[0], width)


def on_device(
    features, w_inner, bias_inner, w_outer, bias_outer, tiles, tile_col, degrees, send_rows
):
    send_lists = send_rows[0]
    classes = w_outer.shape[1]
    padded_width = 128 * ((classes + 127) // 128)
    inv_sqrt = lax.rsqrt(degrees.astype(jnp.float32))[:, None]
    projected = (jnp.dot(features, w_inner, preferred_element_type=jnp.float32) * inv_sqrt).astype(
        jnp.bfloat16
    )
    agg_inner = aggregate(projected, tiles, tile_col, send_lists, deliver_inner)
    hidden = (inv_sqrt * jax.nn.relu(inv_sqrt * agg_inner + bias_inner)).astype(jnp.bfloat16)
    w_padded = jnp.pad(w_outer, ((0, 0), (0, padded_width - classes)))
    scores = jnp.dot(hidden, w_padded, preferred_element_type=jnp.float32).astype(jnp.bfloat16)
    agg_outer = aggregate(scores, tiles, tile_col, send_lists, deliver_outer)
    return inv_sqrt * agg_outer[:, :classes] + bias_outer


def solution(mesh):
    return jax.shard_map(
        on_device,
        mesh=mesh,
        in_specs=(
            P(("dom", "sub"), None),
            P(),
            P(),
            P(),
            P(),
            P(("dom", "sub"), None, None, None),
            P(("dom", "sub"), None),
            P(("dom", "sub")),
            P(("dom", "sub"), None, None),
        ),
        out_specs=P(("dom", "sub"), None),
        check_vma=False,
    )
```

profile of v0, /device:TPU:1, one launch (start us, length us, event | category | flops | bytes accessed | tf_op | source)
XLA Modules:
  0.0 212.0 jit_solution(7271072908278238845)
XLA Ops:
  0.0 0.8 fusion.19
  3.0 1.6 fusion.12
  4.6 16.9 %gather_fusion.2 = bf16[4096,256]{1,0:T(8,128)(2,1)} fusion(bf16[1024,256]{1,0:T(8,128)(2,1)S(1)} %fusion.12, s32[4096]{0:T(1024)S(1)} %fusion.19), kind=kCustom, calls=%fused_computation.2 | custom fusion | bytes 4210688 | tf_op jit(solution)/shard_map/jit(_take)/gather | solution.py:21
  21.5 4.4 %select_select_fusion = bf16[32,128,256]{2,1,0:T(8,128)(2,1)} fusion(bf16[32,128,256]{2,1,0:T(8,128)(2,1)} %bitcast.87, pred[32,128]{1,0:T(8,128)(4,1)S(1)} %compare_and_fusion, pred[32,128]{1,0:T(8,128)(4,1)S(1)} %compare_bitcast_fusion), kind=kLoop, calls=%fused_computation.25 | loop fusion | flops 2097152 | bytes 4202496 | tf_op jit(solution)/shard_map/jit(_where)/select_n | solution.py:20
  25.9 7.1 %all-to-all-start = ((bf16[32,128,256]{2,1,0:T(8,128)(2,1)}), bf16[32,128,256]{2,1,0:T(8,128)(2,1)}, u32[]{:S(2)}, u32[]{:S(2)}) async-start(bf16[32,128,256]{2,1,0:T(8,128)(2,1)} %select_select_fusion), calls=%async_computation | async-start | bytes 4194304 | tf_op jit(solution)/shard_map/all_to_all | solution.py:8
  33.1 48.4 %all-to-all-done = bf16[32,128,256]{2,1,0:T(8,128)(2,1)} async-done(((bf16[32,128,256]{2,1,0:T(8,128)(2,1)}), bf16[32,128,256]{2,1,0:T(8,128)(2,1)}, u32[]{:S(2)}, u32[]{:S(2)}) %all-to-all-start) | async-done | bytes 2097184 | tf_op jit(solution)/shard_map/all_to_all | solution.py:8
  81.4 3.3 %pad_maximum_fusion = bf16[40,128,256]{2,1,0:T(8,128)(2,1)} fusion(bf16[32,128,256]{2,1,0:T(8,128)(2,1)} %all-to-all-done, bf16[8,128,256]{2,1,0:T(8,128)(2,1)S(1)} %bitcast.85), kind=kLoop, calls=%fused_computation.24 | loop fusion | flops 1310720 | bytes 5242880 | tf_op jit(solution)/shard_map/concatenate | solution.py:24
  84.8 43.7 %while.20 = (s32[]{:T(128)}, f32[8,128,256]{2,1,0:T(8,128)}, bf16[8,32,128,128]{3,2,1,0:T(8,128)(2,1)}, s32[8,32]{1,0:T(8,128)}, bf16[40,128,256]{2,1,0:T(8,128)(2,1)}, /*index=5*/s32[]{:T(128)}) while((s32[]{:T(128)}, f32[8,128,256]{2,1,0:T(8,128)}, bf16[8,32,128,128]{3,2,1,0:T(8,128)(2,1)}, s32[8,32]{1,0:T(8,128)}, ...), condition=%wide.region_1.2_spmd, body=%wide.region_0.1_spmd.sunk | while | flops 268436576 | bytes 7476809 | solution.py:31
  85.5 2.4 %gather_fusion = bf16[32,128,256]{2,1,0:T(8,128)(2,1)S(1)} fusion(bf16[40,128,256]{2,1,0:T(8,128)(2,1)} %get-tuple-element.159, s32[1024]{0:T(1024)S(1)} %pad_clamp_fusion.4), kind=kCustom, calls=%fused_computation.clone.1 | custom fusion | bytes 4194432 | tf_op jit(solution)/shard_map/while/body/eval_jaxpr/gather | solution.py:28
  87.9 2.3 %fusion.37 = f32[8,128,256]{2,1,0:T(8,128)} fusion(f32[8,128,256]{2,1,0:T(8,128)} %get-tuple-element.150, s32[]{:T(128)} %get-tuple-element.149, bf16[32,128,256]{2,1,0:T(8,128)(2,1)S(1)} %gather_fusion, bf16[8,32,128,128]{3,2,1,0:T(8,128)(2,1)} %get-tuple-element.157), kind=kOutput, calls=%fused_computation.5.clone.1 | convolution fusion | flops 268435456 | bytes 3277824 | tf_op jit(solution)/shard_map/while/body/eval_jaxpr/tij,tjw->iw/dot_general | solution.py:29
  90.9 2.4 %gather_fusion = bf16[32,128,256]{2,1,0:T(8,128)(2,1)S(1)} fusion(bf16[40,128,256]{2,1,0:T(8,128)(2,1)} %get-tuple-element.159, s32[1024]{0:T(1024)S(1)} %pad_clamp_fusion.4), kind=kCustom, calls=%fused_computation.clone.1 | custom fusion | bytes 4194432 | tf_op jit(solution)/shard_map/while/body/eval_jaxpr/gather | solution.py:28
  93.4 2.3 %fusion.37 = f32[8,128,256]{2,1,0:T(8,128)} fusion(f32[8,128,256]{2,1,0:T(8,128)} %get-tuple-element.150, s32[]{:T(128)} %get-tuple-element.149, bf16[32,128,256]{2,1,0:T(8,128)(2,1)S(1)} %gather_fusion, bf16[8,32,128,128]{3,2,1,0:T(8,128)(2,1)} %get-tuple-element.157), kind=kOutput, calls=%fused_computation.5.clone.1 | convolution fusion | flops 268435456 | bytes 3277824 | tf_op jit(solution)/shard_map/while/body/eval_jaxpr/tij,tjw->iw/dot_general | solution.py:29
  96.4 2.4 %gather_fusion = bf16[32,128,256]{2,1,0:T(8,128)(2,1)S(1)} fusion(bf16[40,128,256]{2,1,0:T(8,128)(2,1)} %get-tuple-element.159, s32[1024]{0:T(1024)S(1)} %pad_clamp_fusion.4), kind=kCustom, calls=%fused_computation.clone.1 | custom fusion | bytes 4194432 | tf_op jit(solution)/shard_map/while/body/eval_jaxpr/gather | solution.py:28
  98.8 2.3 %fusion.37 = f32[8,128,256]{2,1,0:T(8,128)} fusion(f32[8,128,256]{2,1,0:T(8,128)} %get-tuple-element.150, s32[]{:T(128)} %get-tuple-element.149, bf16[32,128,256]{2,1,0:T(8,128)(2,1)S(1)} %gather_fusion, bf16[8,32,128,128]{3,2,1,0:T(8,128)(2,1)} %get-tuple-element.157), kind=kOutput, calls=%fused_computation.5.clone.1 | convolution fusion | flops 268435456 | bytes 3277824 | tf_op jit(solution)/shard_map/while/body/eval_jaxpr/tij,tjw->iw/dot_general | solution.py:29
  101.8 2.4 %gather_fusion = bf16[32,128,256]{2,1,0:T(8,128)(2,1)S(1)} fusion(bf16[40,128,256]{2,1,0:T(8,128)(2,1)} %get-tuple-element.159, s32[1024]{0:T(1024)S(1)} %pad_clamp_fusion.4), kind=kCustom, calls=%fused_computation.clone.1 | custom fusion | bytes 4194432 | tf_op jit(solution)/shard_map/while/body/eval_jaxpr/gather | solution.py:28
  104.3 2.3 %fusion.37 = f32[8,128,256]{2,1,0:T(8,128)} fusion(f32[8,128,256]{2,1,0:T(8,128)} %get-tuple-element.150, s32[]{:T(128)} %get-tuple-element.149, bf16[32,128,256]{2,1,0:T(8,128)(2,1)S(1)} %gather_fusion, bf16[8,32,128,128]{3,2,1,0:T(8,128)(2,1)} %get-tuple-element.157), kind=kOutput, calls=%fused_computation.5.clone.1 | convolution fusion | flops 268435456 | bytes 3277824 | tf_op jit(solution)/shard_map/while/body/eval_jaxpr/tij,tjw->iw/dot_general | solution.py:29
  107.3 2.4 %gather_fusion = bf16[32,128,256]{2,1,0:T(8,128)(2,1)S(1)} fusion(bf16[40,128,256]{2,1,0:T(8,128)(2,1)} %get-tuple-element.159, s32[1024]{0:T(1024)S(1)} %pad_clamp_fusion.4), kind=kCustom, calls=%fused_computation.clone.1 | custom fusion | bytes 4194432 | tf_op jit(solution)/shard_map/while/body/eval_jaxpr/gather | solution.py:28
  109.7 2.3 %fusion.37 = f32[8,128,256]{2,1,0:T(8,128)} fusion(f32[8,128,256]{2,1,0:T(8,128)} %get-tuple-element.150, s32[]{:T(128)} %get-tuple-element.149, bf16[32,128,256]{2,1,0:T(8,128)(2,1)S(1)} %gather_fusion, bf16[8,32,128,128]{3,2,1,0:T(8,128)(2,1)} %get-tuple-element.157), kind=kOutput, calls=%fused_computation.5.clone.1 | convolution fusion | flops 268435456 | bytes 3277824 | tf_op jit(solution)/shard_map/while/body/eval_jaxpr/tij,tjw->iw/dot_general | solution.py:29
  112.7 2.4 %gather_fusion = bf16[32,128,256]{2,1,0:T(8,128)(2,1)S(1)} fusion(bf16[40,128,256]{2,1,0:T(8,128)(2,1)} %get-tuple-element.159, s32[1024]{0:T(1024)S(1)} %pad_clamp_fusion.4), kind=kCustom, calls=%fused_computation.clone.1 | custom fusion | bytes 4194432 | tf_op jit(solution)/shard_map/while/body/eval_jaxpr/gather | solution.py:28
  115.2 2.4 %fusion.37 = f32[8,128,256]{2,1,0:T(8,128)} fusion(f32[8,128,256]{2,1,0:T(8,128)} %get-tuple-element.150, s32[]{:T(128)} %get-tuple-element.149, bf16[32,128,256]{2,1,0:T(8,128)(2,1)S(1)} %gather_fusion, bf16[8,32,128,128]{3,2,1,0:T(8,128)(2,1)} %get-tuple-element.157), kind=kOutput, calls=%fused_computation.5.clone.1 | convolution fusion | flops 268435456 | bytes 3277824 | tf_op jit(solution)/shard_map/while/body/eval_jaxpr/tij,tjw->iw/dot_general | solution.py:29
  118.2 2.4 %gather_fusion = bf16[32,128,256]{2,1,0:T(8,128)(2,1)S(1)} fusion(bf16[40,128,256]{2,1,0:T(8,128)(2,1)} %get-tuple-element.159, s32[1024]{0:T(1024)S(1)} %pad_clamp_fusion.4), kind=kCustom, calls=%fused_computation.clone.1 | custom fusion | bytes 4194432 | tf_op jit(solution)/shard_map/while/body/eval_jaxpr/gather | solution.py:28
  120.7 2.3 %fusion.37 = f32[8,128,256]{2,1,0:T(8,128)} fusion(f32[8,128,256]{2,1,0:T(8,128)} %get-tuple-element.150, s32[]{:T(128)} %get-tuple-element.149, bf16[32,128,256]{2,1,0:T(8,128)(2,1)S(1)} %gather_fusion, bf16[8,32,128,128]{3,2,1,0:T(8,128)(2,1)} %get-tuple-element.157), kind=kOutput, calls=%fused_computation.5.clone.1 | convolution fusion | flops 268435456 | bytes 3277824 | tf_op jit(solution)/shard_map/while/body/eval_jaxpr/tij,tjw->iw/dot_general | solution.py:29
  123.7 2.4 %gather_fusion = bf16[32,128,256]{2,1,0:T(8,128)(2,1)S(1)} fusion(bf16[40,128,256]{2,1,0:T(8,128)(2,1)} %get-tuple-element.159, s32[1024]{0:T(1024)S(1)} %pad_clamp_fusion.4), kind=kCustom, calls=%fused_computation.clone.1 | custom fusion | bytes 4194432 | tf_op jit(solution)/shard_map/while/body/eval_jaxpr/gather | solution.py:28
  126.1 2.3 %fusion.37 = f32[8,128,256]{2,1,0:T(8,128)} fusion(f32[8,128,256]{2,1,0:T(8,128)} %get-tuple-element.150, s32[]{:T(128)} %get-tuple-element.149, bf16[32,128,256]{2,1,0:T(8,128)(2,1)S(1)} %gather_fusion, bf16[8,32,128,128]{3,2,1,0:T(8,128)(2,1)} %get-tuple-element.157), kind=kOutput, calls=%fused_computation.5.clone.1 | convolution fusion | flops 268435456 | bytes 3277824 | tf_op jit(solution)/shard_map/while/body/eval_jaxpr/tij,tjw->iw/dot_general | solution.py:29
  128.5 1.4 fusion.16
  130.2 12.1 %gather_fusion.3 = bf16[4096,128]{1,0:T(8,128)(2,1)S(1)} fusion(bf16[1024,128]{1,0:T(8,128)(2,1)S(1)} %convolution_convert_fusion, s32[4096]{0:T(1024)S(1)} %fusion.19), kind=kCustom, calls=%fused_computation.3 | custom fusion | bytes 2113536 | tf_op jit(solution)/shard_map/jit(_take)/gather | solution.py:21
  142.3 2.4 %select_select_fusion.1 = bf16[32,128,128]{2,1,0:T(8,128)(2,1)} fusion(bf16[32,128,128]{2,1,0:T(8,128)(2,1)S(1)} %bitcast.88, pred[32,128]{1,0:T(8,128)(4,1)S(1)} %compare_and_fusion, pred[32,128]{1,0:T(8,128)(4,1)S(1)} %compare_bitcast_fusion), kind=kLoop, calls=%fused_computation.35 | loop fusion | flops 1048576 | bytes 2105344 | tf_op jit(solution)/shard_map/jit(_where)/select_n | solution.py:20
  144.8 3.2 %all-to-all-start.1 = ((bf16[32,128,128]{2,1,0:T(8,128)(2,1)}), bf16[32,128,128]{2,1,0:T(8,128)(2,1)S(1)}, u32[]{:S(2)}, u32[]{:S(2)}) async-start(bf16[32,128,128]{2,1,0:T(8,128)(2,1)} %select_select_fusion.1), calls=%async_computation.1 | async-start | bytes 2097152 | tf_op jit(solution)/shard_map/all_to_all | solution.py:12
  147.9 26.3 %all-to-all-done.1 = bf16[32,128,128]{2,1,0:T(8,128)(2,1)S(1)} async-done(((bf16[32,128,128]{2,1,0:T(8,128)(2,1)}), bf16[32,128,128]{2,1,0:T(8,128)(2,1)S(1)}, u32[]{:S(2)}, u32[]{:S(2)}) %all-to-all-start.1) | async-done | bytes 1048608 | tf_op jit(solution)/shard_map/all_to_all | solution.py:12
  174.3 1.2 pad_maximum_fusion.1
  175.5 35.6 %while.21 = (s32[]{:T(128)}, f32[8,128,128]{2,1,0:T(8,128)S(1)}, bf16[8,32,128,128]{3,2,1,0:T(8,128)(2,1)}, s32[8,32]{1,0:T(8,128)}, bf16[40,128,128]{2,1,0:T(8,128)(2,1)}, /*index=5*/s32[]{:T(128)}) while((s32[]{:T(128)}, f32[8,128,128]{2,1,0:T(8,128)S(1)}, bf16[8,32,128,128]{3,2,1,0:T(8,128)(2,1)}, s32[8,32]{1,0:T(8,128)}, ...), condition=%wide.region_3.4_spmd, body=%wide.region_2.3_spmd.sunk | while | flops 134218848 | bytes 4265545 | solution.py:31
  176.2 2.1 gather_fusion.1
  178.2 1.7 fusion.41
  180.6 2.1 gather_fusion.1
  182.7 1.7 fusion.41
  185.1 2.1 gather_fusion.1
  187.1 1.7 fusion.41
  189.5 2.1 gather_fusion.1
  191.6 1.7 fusion.41
  194.0 2.1 gather_fusion.1
  196.0 1.7 fusion.41
  198.4 2.1 gather_fusion.1
  200.5 1.7 fusion.41
  202.9 2.1 gather_fusion.1
  204.9 1.7 fusion.41
  207.3 2.1 gather_fusion.1
  209.4 1.7 fusion.41
  211.3 0.8 multiply_add_fusion
  (47 shorter events, 13.9 us)
Async XLA Ops:
  0.0 3.0 %copy-start = (bf16[1024,602]{0,1:T(8,128)(2,1)S(1)}, bf16[1024,602]{0,1:T(8,128)(2,1)}, u32[]{:S(2)}) copy-start(bf16[1024,602]{0,1:T(8,128)(2,1)} %param.13) | copy-start | bytes 3698692
  25.9 55.5 %all-to-all-start = ((bf16[32,128,256]{2,1,0:T(8,128)(2,1)}), bf16[32,128,256]{2,1,0:T(8,128)(2,1)}, u32[]{:S(2)}, u32[]{:S(2)}) async-start(bf16[32,128,256]{2,1,0:T(8,128)(2,1)} %select_select_fusion), calls=%async_computation | async-start | bytes 4194304 | tf_op jit(solution)/shard_map/all_to_all | solution.py:8
  84.8 43.7 %copy-start.2 = (f32[256]{0:T(256)S(1)}, f32[256]{0:T(256)}, u32[]{:S(2)}) copy-start(f32[256]{0:T(256)} %param.15) | copy-start | bytes 3076
  84.8 45.2 %copy-start.1 = (bf16[256,41]{0,1:T(8,128)(2,1)S(1)}, bf16[256,41]{0,1:T(8,128)(2,1)}, u32[]{:S(2)}) copy-start(bf16[256,41]{0,1:T(8,128)(2,1)} %param.16) | copy-start | bytes 62980
  144.8 29.5 %all-to-all-start.1 = ((bf16[32,128,128]{2,1,0:T(8,128)(2,1)}), bf16[32,128,128]{2,1,0:T(8,128)(2,1)S(1)}, u32[]{:S(2)}, u32[]{:S(2)}) async-start(bf16[32,128,128]{2,1,0:T(8,128)(2,1)} %select_select_fusion.1), calls=%async_computation.1 | async-start | bytes 2097152 | tf_op jit(solution)/shard_map/all_to_all | solution.py:12
  175.5 35.8 %copy-start.3 = (f32[41]{0:T(128)S(1)}, f32[41]{0:T(128)}, u32[]{:S(2)}) copy-start(f32[41]{0:T(128)} %param.17) | copy-start | bytes 496
where the time goes:
time: 214 us; the launch traced here: 212 us
  waiting for transfers between devices  74.7 us (35%)
  local copies, waits for them, and re-layouts  65.1 us (30%)
  matrix products  33.7 us (16%)
  other arithmetic  27.8 us (13%)
  starting transfers between devices  10.3 us (5%)
    all_to_all x1, waiting for transfers between devices, deliver_inner(): lax.all_to_all(outgoing, ('dom', 'sub'), split_axis=0, concat_axis=0, til...  48.4 us
    gather x16, local copies, waits for them, and re-layouts, rowblock(): blocks = columns[col_set]  35.9 us
    dot_general x16, matrix products, rowblock(): jnp.einsum('tij,tjw->iw', tile_set, blocks, preferred_element_type=jnp.fl...  31.8 us
    gather x2, local copies, waits for them, and re-layouts, aggregate(): jnp.take(feature_rows, clipped, axis=0)  29.1 us
    all_to_all x1, waiting for transfers between devices, deliver_outer(): lax.all_to_all(outgoing, ('dom', 'sub'), split_axis=0, concat_axis=0, til...  26.3 us
    select_n x16, other arithmetic, rowblock(): blocks = columns[col_set]  11.1 us
    all_to_all x1, starting transfers between devices, deliver_inner(): lax.all_to_all(outgoing, ('dom', 'sub'), split_axis=0, concat_axis=0, til...  7.14 us
    select_n x2, other arithmetic, aggregate(): jnp.where(live_slot, jnp.take(feature_rows, clipped, axis=0), jnp.zeros((...  6.83 us
  transfers between devices with their start and end apart: 2, of which 2 were waited for; matrix products, arithmetic and copies ran while one was open for 0% of the time, Pallas kernels for 0%

commit v1 on v0

v1 whole, which is shorter than its diff:
```python
import functools

import jax
import jax.numpy as jnp
from jax import lax
from jax.experimental import pallas as pl
from jax.experimental.pallas import tpu as pltpu
from jax.sharding import PartitionSpec as P

AXES = ("dom", "sub")
NT = (((1,), (1,)), ((), ()))
TN = (((0,), (0,)), ((), ()))
SMEM = pl.BlockSpec(memory_space=pltpu.SMEM)
VMEM = pl.BlockSpec(memory_space=pltpu.VMEM)
ANY = pl.BlockSpec(memory_space=pl.ANY)


def one_hot_rows(slots, rows):
    lane = lax.broadcasted_iota(jnp.int32, (slots.shape[0], rows), 1)
    return jnp.where(slots == lane, 1.0, 0.0).astype(jnp.bfloat16)


def one_hot_cols(slots, rows):
    sub = lax.broadcasted_iota(jnp.int32, (rows, slots.shape[1]), 0)
    return jnp.where(slots == sub, 1.0, 0.0).astype(jnp.bfloat16)


def inv_sqrt_columns(deg_ref):
    return jnp.transpose(lax.rsqrt(deg_ref[...].astype(jnp.float32)))


def project_kernel(feat_ref, w_ref, deg_ref, send_ref, proj_ref, out_ref):
    blocks, blk, _ = proj_ref.shape
    rows = blocks * blk

    @pl.when(pl.program_id(0) == 0)
    def _():
        inv = inv_sqrt_columns(deg_ref)
        for b in range(blocks):
            part = lax.dot_general(
                feat_ref[:, b * blk : (b + 1) * blk],
                w_ref[...],
                TN,
                preferred_element_type=jnp.float32,
            )
            proj_ref[b] = (part * inv[:, b : b + 1]).astype(proj_ref.dtype)

    slots = jnp.transpose(send_ref[...])
    table = proj_ref[...].reshape(rows, proj_ref.shape[2])
    for p in range(out_ref.shape[0]):
        picked = jnp.dot(
            one_hot_rows(slots[:, p : p + 1], rows), table, preferred_element_type=jnp.float32
        )
        out_ref[p] = picked.astype(out_ref.dtype)


def project_and_pick(feat_t, w_inner, deg, send_lists):
    f_in, rows = feat_t.shape
    hid = w_inner.shape[1]
    peers, blk = send_lists.shape
    blocks = rows // blk
    chunk = 8 if peers % 8 == 0 else peers
    return pl.pallas_call(
        project_kernel,
        grid=(peers // chunk,),
        in_specs=[
            pl.BlockSpec((f_in, rows), lambda g: (0, 0)),
            pl.BlockSpec((f_in, hid), lambda g: (0, 0)),
            pl.BlockSpec((blocks, blk), lambda g: (0, 0)),
            pl.BlockSpec((chunk, blk), lambda g: (g, 0)),
        ],
        out_specs=[
            pl.BlockSpec((blocks, blk, hid), lambda g: (0, 0, 0)),
            pl.BlockSpec((chunk, blk, hid), lambda g: (g, 0, 0)),
        ],
        out_shape=[
            jax.ShapeDtypeStruct((blocks, blk, hid), jnp.bfloat16),
            jax.ShapeDtypeStruct((peers, blk, hid), jnp.bfloat16),
        ],
        name="project_pick",
    )(feat_t, w_inner, deg, send_lists)


def start_fetches(own, arrived, tiles, columns, tiles_v, sems):
    own_blocks = own.shape[0]
    row_blocks = tiles.shape[0]
    first = pltpu.make_async_copy(own, columns.at[pl.ds(0, own_blocks)], sems.at[0])
    second = pltpu.make_async_copy(
        arrived, columns.at[pl.ds(own_blocks, arrived.shape[0])], sems.at[1]
    )
    sets = [
        pltpu.make_async_copy(tiles.at[r], tiles_v.at[r], sems.at[2 + r]) for r in range(row_blocks)
    ]
    for copy in [first, second] + sets:
        copy.start()

    def wait_columns():
        first.wait()
        second.wait()

    return wait_columns, [copy.wait for copy in sets]


def inner_kernel(
    col_ref, own, arrived, tiles, deg_ref, bias_ref, wt_ref, send_ref,
    scores_ref, out_ref, columns, tiles_v, table, sems,
):
    row_blocks, per_row, blk, _ = tiles.shape
    peers = send_ref.shape[0]
    rows = row_blocks * blk
    wait_columns, wait_tiles = start_fetches(own, arrived, tiles, columns, tiles_v, sems)
    inv = inv_sqrt_columns(deg_ref)
    wait_columns()
    for r in range(row_blocks):
        wait_tiles[r]()
        total = jnp.zeros((blk, columns.shape[2]), jnp.float32)
        for t in range(0, per_row, 2):
            left = jnp.concatenate([tiles_v[r, t], tiles_v[r, t + 1]], axis=1)
            right = jnp.concatenate([columns[col_ref[r, t]], columns[col_ref[r, t + 1]]], axis=0)
            total = total + jnp.dot(left, right, preferred_element_type=jnp.float32)
        scale = inv[:, r : r + 1]
        hidden = (scale * jax.nn.relu(scale * total + bias_ref[...])).astype(jnp.bfloat16)
        scores = lax.dot_general(wt_ref[...], hidden, NT, preferred_element_type=jnp.float32)
        scores = scores.astype(jnp.bfloat16)
        scores_ref[r] = scores
        table[:, r * blk : (r + 1) * blk] = scores

    def pick(step, carry):
        base = step * 4
        for half in range(2):
            p = base + 2 * half
            slots = jnp.concatenate([send_ref[pl.ds(p, 1)], send_ref[pl.ds(p + 1, 1)]], axis=1)
            picked = jnp.dot(
                table[...], one_hot_cols(slots, rows), preferred_element_type=jnp.float32
            ).astype(out_ref.dtype)
            out_ref[p] = picked[:, :blk]
            out_ref[p + 1] = picked[:, blk:]
        return carry

    lax.fori_loop(0, peers // 4, pick, 0)


def aggregate_inner(tile_col, own, arrived, tiles, deg, bias, w_t, send_lists):
    classes = w_t.shape[0]
    blocks, blk, hid = own.shape
    peers = arrived.shape[0]
    return pl.pallas_call(
        inner_kernel,
        in_specs=[SMEM, ANY, ANY, ANY, VMEM, VMEM, VMEM, VMEM],
        out_specs=[VMEM, VMEM],
        out_shape=[
            jax.ShapeDtypeStruct((blocks, classes, blk), jnp.bfloat16),
            jax.ShapeDtypeStruct((peers, classes, blk), jnp.bfloat16),
        ],
        scratch_shapes=[
            pltpu.VMEM((blocks + peers, blk, hid), jnp.bfloat16),
            pltpu.VMEM(tiles.shape, jnp.bfloat16),
            pltpu.VMEM((classes, blocks * blk), jnp.bfloat16),
            pltpu.SemaphoreType.DMA((2 + blocks,)),
        ],
        name="aggregate_inner",
    )(tile_col, own, arrived, tiles, deg, bias, w_t, send_lists)


def outer_kernel(
    col_ref, own, arrived, tiles, deg_ref, bias_ref, out_ref, columns, tiles_v, sems
):
    row_blocks, per_row, blk, _ = tiles.shape
    classes = out_ref.shape[0]
    wait_columns, wait_tiles = start_fetches(own, arrived, tiles, columns, tiles_v, sems)
    inv = lax.rsqrt(deg_ref[...].astype(jnp.float32))
    square = (classes, classes)
    diagonal = lax.broadcasted_iota(jnp.int32, square, 0) == lax.broadcasted_iota(jnp.int32, square, 1)
    bias = jnp.sum(jnp.where(diagonal, bias_ref[...], 0.0), axis=1, keepdims=True)
    wait_columns()
    for r in range(row_blocks):
        wait_tiles[r]()
        total = jnp.zeros((classes, blk), jnp.float32)
        for t in range(0, per_row, 2):
            left = jnp.concatenate([columns[col_ref[r, t]], columns[col_ref[r, t + 1]]], axis=1)
            right = jnp.concatenate([tiles_v[r, t], tiles_v[r, t + 1]], axis=1)
            total = total + lax.dot_general(left, right, NT, preferred_element_type=jnp.float32)
        out_ref[:, r * blk : (r + 1) * blk] = inv[r : r + 1] * total + bias


def aggregate_outer(tile_col, own, arrived, tiles, deg, bias):
    blocks, classes, blk = own.shape
    peers = arrived.shape[0]
    return pl.pallas_call(
        outer_kernel,
        in_specs=[SMEM, ANY, ANY, ANY, VMEM, VMEM],
        out_specs=VMEM,
        out_shape=jax.ShapeDtypeStruct((classes, blocks * blk), jnp.float32),
        scratch_shapes=[
            pltpu.VMEM((blocks + peers, classes, blk), jnp.bfloat16),
            pltpu.VMEM(tiles.shape, jnp.bfloat16),
            pltpu.SemaphoreType.DMA((2 + blocks,)),
        ],
        name="aggregate_outer",
    )(tile_col, own, arrived, tiles, deg, bias)


def exchange(outgoing):
    return lax.all_to_all(outgoing, AXES, split_axis=0, concat_axis=0, tiled=True)


def on_device(
    features, w_inner, bias_inner, w_outer, bias_outer, tiles, tile_col, degrees, send_rows
):
    send_lists = send_rows[0]
    deg = degrees.reshape(-1, tiles.shape[2])
    own, outgoing = project_and_pick(features.T, w_inner, deg, send_lists)
    arrived = exchange(outgoing)
    own_scores, outgoing = aggregate_inner(
        tile_col, own, arrived, tiles, deg, bias_inner[None], w_outer.T, send_lists
    )
    arrived = exchange(outgoing)
    return aggregate_outer(tile_col, own_scores, arrived, tiles, deg, bias_outer[None]).T


def solution(mesh):
    return jax.shard_map(
        on_device,
        mesh=mesh,
        in_specs=(
            P(AXES, None),
            P(),
            P(),
            P(),
            P(),
            P(AXES, None, None, None),
            P(AXES, None),
            P(AXES),
            P(AXES, None, None),
        ),
        out_specs=P(AXES, None),
        check_vma=False,
    )
```

time: 214 us -> 101 us (0.47)
  waiting for transfers between devices: 74.7 us -> 0 us
  blocking collectives: 0 us -> 72.1 us
  local copies, waits for them, and re-layouts: 65.1 us -> 0 us
  matrix products: 33.7 us -> 0 us
  Pallas kernels: 0 us -> 28.1 us
  other arithmetic: 27.8 us -> 0 us
  starting transfers between devices: 10.3 us -> 0 us
    all_to_all x2 -> x0, waiting for transfers between devices: 74.7 us -> none  [the longest x1 48.4 us: deliver_inner(): lax.all_to_all(outgoing, ('dom', 'sub'), split_axis=0, concat_axis=0, til...]
    all_to_all x0 -> x2, blocking collectives: none -> 72.1 us  [exchange(): lax.all_to_all(outgoing, AXES, split_axis=0, concat_axis=0, tiled=True)]
    gather x18 -> x0, local copies, waits for them, and re-layouts: 64.9 us -> none  [the longest x16 35.9 us: rowblock(): blocks = columns[col_set]]
    dot_general x18 -> x0, matrix products: 33.7 us -> none  [the longest x16 31.8 us: rowblock(): jnp.einsum('tij,tjw->iw', tile_set, blocks, preferred_element_type=jnp.fl...]
    pallas_call x0 -> x3, Pallas kernels: none -> 28.1 us  [the longest x1 12.7 us: aggregate_inner(): pl.pallas_call(inner_kernel, in_specs=[SMEM, ANY, ANY, ANY, VMEM, VMEM, V...]
    select_n x18 -> x0, other arithmetic: 18 us -> none  [the longest x16 11.1 us: rowblock(): blocks = columns[col_set]]
    all_to_all x2 -> x0, starting transfers between devices: 10.3 us -> none  [the longest x1 7.14 us: deliver_inner(): lax.all_to_all(outgoing, ('dom', 'sub'), split_axis=0, concat_axis=0, til...]
    concatenate x2 -> x0, other arithmetic: 4.52 us -> none  [aggregate(): jnp.concatenate([feature_rows.reshape(-1, block_rows, width), arrived], a...]
  transfers between devices with their start and end apart: 2 -> 0, of which waited for: 2 -> 0; matrix products, arithmetic and copies ran while one was open for 0% -> 0% of each run, Pallas kernels for 0% -> 0%
where the time goes in v1:
time: 101 us; the launch traced here: 100 us
  blocking collectives  72.1 us (71%)
  Pallas kernels  28.1 us (28%)
    all_to_all x2, blocking collectives, exchange(): lax.all_to_all(outgoing, AXES, split_axis=0, concat_axis=0, tiled=True)  72.1 us
    pallas_call x1, Pallas kernels, aggregate_inner(): pl.pallas_call(inner_kernel, in_specs=[SMEM, ANY, ANY, ANY, VMEM, VMEM, V...  12.7 us
    pallas_call x1, Pallas kernels, aggregate_outer(): pl.pallas_call(outer_kernel, in_specs=[SMEM, ANY, ANY, ANY, VMEM, VMEM],...  8.23 us
    pallas_call x1, Pallas kernels, project_and_pick(): pl.pallas_call(project_kernel, grid=(peers // chunk,), in_specs=[pl.Block...  7.19 us

profile of v1, /device:TPU:1, one launch (start us, length us, event | category | flops | bytes accessed | tf_op | source)
XLA Modules:
  0.0 100.2 jit_solution(14316882330242887638)
XLA Ops:
  0.0 7.2 %project_pick.1 = (bf16[8,128,256]{2,1,0:T(8,128)(2,1)}, bf16[32,128,256]{2,1,0:T(8,128)(2,1)}) custom-call(bf16[602,1024]{1,0:T(8,128)(2,1)} %bitcast.7, bf16[602,256]{1,0:T(8,128)(2,1)} %w_ref.1, s32[8,128]{1,0:T(8,128)} %bitcast.10, s32[32,128]{1,0:T(8,128)} %bitcast.8), custom_call_target="tpu_custom_call" | custom-call | tf_op jit(solution)/shard_map/project_pick/pallas_call | solution.py:63
  7.2 56.0 %all_to_all.10.arrived = bf16[32,128,256]{2,1,0:T(8,128)(2,1)} all-to-all(bf16[32,128,256]{2,1,0:T(8,128)(2,1)} %get-tuple-element.10), channel_id=1, replica_groups=mesh['dom'=8,'sub'=4] {'dom','sub'}, dimensions={0} | all-to-all | bytes 4194304 | tf_op jit(solution)/shard_map/all_to_all | solution.py:204
  63.2 12.7 %aggregate_inner.1 = (bf16[8,41,128]{2,1,0:T(8,128)(2,1)}, bf16[32,41,128]{2,1,0:T(8,128)(2,1)}) custom-call(s32[8,32]{1,0:T(8,128)} %col_ref.3, bf16[8,128,256]{2,1,0:T(8,128)(2,1)} %get-tuple-element.9.own, bf16[32,128,256]{2,1,0:T(8,128)(2,1)} %all_to_all.10.arrived, bf16[8,32,128,128]{3,2,1,0:T(8,128)(2,1)} %tiles.3, s32[8,128]{1,0:T(8,128)} %bitcast.11, ...), custom_call_target="tpu_custom_call" | custom-call | tf_op jit(solution)/shard_map/aggregate_inner/pallas_call | solution.py:147
  75.9 16.1 %all_to_all.11.arrived = bf16[32,41,128]{2,1,0:T(8,128)(2,1)} all-to-all(bf16[32,41,128]{2,1,0:T(8,128)(2,1)} %get-tuple-element.12), channel_id=1, replica_groups=mesh['dom'=8,'sub'=4] {'dom','sub'}, dimensions={0} | all-to-all | bytes 671744 | tf_op jit(solution)/shard_map/all_to_all | solution.py:204
  92.0 8.2 %aggregate_outer.1 = f32[41,1024]{1,0:T(8,128)} custom-call(s32[8,32]{1,0:T(8,128)} %col_ref.3, bf16[8,41,128]{2,1,0:T(8,128)(2,1)} %get-tuple-element.11.own, bf16[32,41,128]{2,1,0:T(8,128)(2,1)} %all_to_all.11.arrived, bf16[8,32,128,128]{3,2,1,0:T(8,128)(2,1)} %tiles.3, s32[8,128]{1,0:T(8,128)} %bitcast.12, f32[1,41]{1,0:T(1,128)} %bitcast.15), custom_call_target="tpu_custom_call" | custom-call | tf_op jit(solution)/shard_map/aggregate_outer/pallas_call | solution.py:189

commit v2 on v1

--- a/solution.py
+++ b/solution.py
@@ -101,6 +101,29 @@
     return wait_columns, [copy.wait for copy in sets]
 
 
+def row_block_sum(tiles_v, columns, col_ref, r, product):
+    total = None
+    for t in range(0, tiles_v.shape[1], 2):
+        left = jnp.concatenate([tiles_v[r, t], tiles_v[r, t + 1]], axis=1)
+        part = product(left, columns[col_ref[r, t]], columns[col_ref[r, t + 1]])
+        total = part if total is None else total + part
+    return total
+
+
+def row_blocks_in_pairs(row_blocks, wait_tiles, block_sum, finish):
+    ready = []
+    for first in range(0, row_blocks, 2):
+        pair = range(first, min(first + 2, row_blocks))
+        for r in pair:
+            wait_tiles[r]()
+        sums = [(r, block_sum(r)) for r in pair]
+        for done in ready:
+            finish(*done)
+        ready = sums
+    for done in ready:
+        finish(*done)
+
+
 def inner_kernel(
     col_ref, own, arrived, tiles, deg_ref, bias_ref, wt_ref, send_ref,
     scores_ref, out_ref, columns, tiles_v, table, sems,
@@ -110,20 +133,24 @@
     rows = row_blocks * blk
     wait_columns, wait_tiles = start_fetches(own, arrived, tiles, columns, tiles_v, sems)
     inv = inv_sqrt_columns(deg_ref)
-    wait_columns()
-    for r in range(row_blocks):
-        wait_tiles[r]()
-        total = jnp.zeros((blk, columns.shape[2]), jnp.float32)
-        for t in range(0, per_row, 2):
-            left = jnp.concatenate([tiles_v[r, t], tiles_v[r, t + 1]], axis=1)
-            right = jnp.concatenate([columns[col_ref[r, t]], columns[col_ref[r, t + 1]]], axis=0)
-            total = total + jnp.dot(left, right, preferred_element_type=jnp.float32)
+
+    def finish(r, total):
         scale = inv[:, r : r + 1]
         hidden = (scale * jax.nn.relu(scale * total + bias_ref[...])).astype(jnp.bfloat16)
         scores = lax.dot_general(wt_ref[...], hidden, NT, preferred_element_type=jnp.float32)
         scores = scores.astype(jnp.bfloat16)
         scores_ref[r] = scores
         table[:, r * blk : (r + 1) * blk] = scores
+
+    def block_sum(r):
+        return row_block_sum(
+            tiles_v, columns, col_ref, r, lambda left, a, b: jnp.dot(
+                left, jnp.concatenate([a, b], axis=0), preferred_element_type=jnp.float32
+            )
+        )
+
+    wait_columns()
+    row_blocks_in_pairs(row_blocks, wait_tiles, block_sum, finish)
 
     def pick(step, carry):
         base = step * 4
@@ -172,15 +199,18 @@
     square = (classes, classes)
     diagonal = lax.broadcasted_iota(jnp.int32, square, 0) == lax.broadcasted_iota(jnp.int32, square, 1)
     bias = jnp.sum(jnp.where(diagonal, bias_ref[...], 0.0), axis=1, keepdims=True)
+    def block_sum(r):
+        return row_block_sum(
+            tiles_v, columns, col_ref, r, lambda left, a, b: lax.dot_general(
+                left, jnp.concatenate([a, b], axis=1), NT, preferred_element_type=jnp.float32
+            )
+        )
+
+    def finish(r, total):
+        out_ref[:, r * blk : (r + 1) * blk] = inv[r : r + 1] * jnp.transpose(total) + bias
+
     wait_columns()
-    for r in range(row_blocks):
-        wait_tiles[r]()
-        total = jnp.zeros((classes, blk), jnp.float32)
-        for t in range(0, per_row, 2):
-            left = jnp.concatenate([columns[col_ref[r, t]], columns[col_ref[r, t + 1]]], axis=1)
-            right = jnp.concatenate([tiles_v[r, t], tiles_v[r, t + 1]], axis=1)
-            total = total + lax.dot_general(left, right, NT, preferred_element_type=jnp.float32)
-        out_ref[:, r * blk : (r + 1) * blk] = inv[r : r + 1] * total + bias
+    row_blocks_in_pairs(row_blocks, wait_tiles, block_sum, finish)
 
 
 def aggregate_outer(tile_col, own, arrived, tiles, deg, bias):

time: 101 us -> 95.2 us (0.943)
  Pallas kernels: 28.1 us -> 22.7 us
    pallas_call x1, Pallas kernels: 12.7 us -> 9.49 us  [aggregate_inner(): pl.pallas_call(inner_kernel, in_specs=[SMEM, ANY, ANY, ANY, VMEM, VMEM, V...]
    pallas_call x1, Pallas kernels: 8.23 us -> 6.02 us  [aggregate_outer(): pl.pallas_call(outer_kernel, in_specs=[SMEM, ANY, ANY, ANY, VMEM, VMEM],...]
where the time goes in v2:
time: 95.2 us; the launch traced here: 94.8 us
  blocking collectives  72.1 us (76%)
  Pallas kernels  22.7 us (24%)
    all_to_all x2, blocking collectives, exchange(): lax.all_to_all(outgoing, AXES, split_axis=0, concat_axis=0, tiled=True)  72.1 us
    pallas_call x1, Pallas kernels, aggregate_inner(): pl.pallas_call(inner_kernel, in_specs=[SMEM, ANY, ANY, ANY, VMEM, VMEM, V...  9.49 us
    pallas_call x1, Pallas kernels, project_and_pick(): pl.pallas_call(project_kernel, grid=(peers // chunk,), in_specs=[pl.Block...  7.19 us
    pallas_call x1, Pallas kernels, aggregate_outer(): pl.pallas_call(outer_kernel, in_specs=[SMEM, ANY, ANY, ANY, VMEM, VMEM],...  6.02 us

profile of v2, /device:TPU:1, one launch (start us, length us, event | category | flops | bytes accessed | tf_op | source)
XLA Modules:
  0.0 94.8 jit_solution(15019207487839311711)
XLA Ops:
  0.0 7.2 %project_pick.1 = (bf16[8,128,256]{2,1,0:T(8,128)(2,1)}, bf16[32,128,256]{2,1,0:T(8,128)(2,1)}) custom-call(bf16[602,1024]{1,0:T(8,128)(2,1)} %bitcast.7, bf16[602,256]{1,0:T(8,128)(2,1)} %w_ref.1, s32[8,128]{1,0:T(8,128)} %bitcast.10, s32[32,128]{1,0:T(8,128)} %bitcast.8), custom_call_target="tpu_custom_call" | custom-call | tf_op jit(solution)/shard_map/project_pick/pallas_call | solution.py:63
  7.2 56.0 %all_to_all.10.arrived = bf16[32,128,256]{2,1,0:T(8,128)(2,1)} all-to-all(bf16[32,128,256]{2,1,0:T(8,128)(2,1)} %get-tuple-element.10), channel_id=1, replica_groups=mesh['dom'=8,'sub'=4] {'dom','sub'}, dimensions={0} | all-to-all | bytes 4194304 | tf_op jit(solution)/shard_map/all_to_all | solution.py:234
  63.2 9.5 %aggregate_inner.1 = (bf16[8,41,128]{2,1,0:T(8,128)(2,1)}, bf16[32,41,128]{2,1,0:T(8,128)(2,1)}) custom-call(s32[8,32]{1,0:T(8,128)} %col_ref.3, bf16[8,128,256]{2,1,0:T(8,128)(2,1)} %get-tuple-element.9.own, bf16[32,128,256]{2,1,0:T(8,128)(2,1)} %all_to_all.10.arrived, bf16[8,32,128,128]{3,2,1,0:T(8,128)(2,1)} %tiles.3, s32[8,128]{1,0:T(8,128)} %bitcast.11, ...), custom_call_target="tpu_custom_call" | custom-call | tf_op jit(solution)/shard_map/aggregate_inner/pallas_call | solution.py:174
  72.7 16.1 %all_to_all.11.arrived = bf16[32,41,128]{2,1,0:T(8,128)(2,1)} all-to-all(bf16[32,41,128]{2,1,0:T(8,128)(2,1)} %get-tuple-element.12), channel_id=1, replica_groups=mesh['dom'=8,'sub'=4] {'dom','sub'}, dimensions={0} | all-to-all | bytes 671744 | tf_op jit(solution)/shard_map/all_to_all | solution.py:234
  88.8 6.0 %aggregate_outer.1 = f32[41,1024]{1,0:T(8,128)} custom-call(s32[8,32]{1,0:T(8,128)} %col_ref.3, bf16[8,41,128]{2,1,0:T(8,128)(2,1)} %get-tuple-element.11.own, bf16[32,41,128]{2,1,0:T(8,128)(2,1)} %all_to_all.11.arrived, bf16[8,32,128,128]{3,2,1,0:T(8,128)(2,1)} %tiles.3, s32[8,128]{1,0:T(8,128)} %bitcast.12, f32[1,41]{1,0:T(1,128)} %bitcast.15), custom_call_target="tpu_custom_call" | custom-call | tf_op jit(solution)/shard_map/aggregate_outer/pallas_call | solution.py:219

commit v3 on v2

v3 whole, which is shorter than its diff:
```python
import functools

import jax
import jax.numpy as jnp
from jax import lax
from jax.experimental import pallas as pl
from jax.experimental.pallas import tpu as pltpu
from jax.sharding import Mesh
from jax.sharding import PartitionSpec as P

NT = (((1,), (1,)), ((), ()))
TN = (((0,), (0,)), ((), ()))
SMEM = pl.BlockSpec(memory_space=pltpu.SMEM)
VMEM = pl.BlockSpec(memory_space=pltpu.VMEM)
ANY = pl.BlockSpec(memory_space=pl.ANY)
HBM = pl.BlockSpec(memory_space=pltpu.HBM)
ROOMY = pltpu.CompilerParams(vmem_limit_bytes=58 * 2**20)
SMALL = pltpu.CompilerParams(vmem_limit_bytes=24 * 2**20)
LIST_BITS = 5
RIGHT_BLOCKS = 5


def one_hot_rows(slots, rows):
    lane = lax.broadcasted_iota(jnp.int32, (slots.shape[0], rows), 1)
    return jnp.where(slots == lane, 1.0, 0.0).astype(jnp.bfloat16)


def one_hot_cols(slots, rows):
    sub = lax.broadcasted_iota(jnp.int32, (rows, slots.shape[1]), 0)
    return jnp.where(slots == sub, 1.0, 0.0).astype(jnp.bfloat16)


def inv_sqrt_columns(deg_ref):
    return jnp.transpose(lax.rsqrt(deg_ref[...].astype(jnp.float32)))


def half_lists(send_ref, side, groups):
    run = send_ref.shape[0] // (2 * groups)
    runs = []
    for g in range(groups):
        low = send_ref[2 * g * run : (2 * g + 1) * run]
        high = send_ref[(2 * g + 1) * run : (2 * g + 2) * run]
        runs.append(jnp.where(side == 0, low, high))
    return jnp.concatenate(runs, axis=0)


def project_kernel(
    side_ref, feat_ref, w_ref, deg_ref, send_ref, left_ref, right_ref, slots_ref, *, groups
):
    blocks, blk = deg_ref.shape
    left_rows = blocks * blk - right_ref.shape[0]
    inv = inv_sqrt_columns(deg_ref)
    for b in range(blocks):
        part = lax.dot_general(
            feat_ref[:, b * blk : (b + 1) * blk],
            w_ref[...],
            TN,
            preferred_element_type=jnp.float32,
        )
        part = (part * inv[:, b : b + 1]).astype(left_ref.dtype)
        if b * blk < left_rows:
            left_ref[b * blk : (b + 1) * blk, :] = part
        else:
            right_ref[b * blk - left_rows : (b + 1) * blk - left_rows, :] = part
    side = side_ref[0]
    lists = half_lists(send_ref, 1 - side, groups)
    coded = jnp.concatenate([lists >> LIST_BITS, lists & (2**LIST_BITS - 1)], axis=1)
    left_ref[left_rows:, :] = coded.astype(jnp.float32).astype(left_ref.dtype)
    slots_ref[...] = jnp.transpose(half_lists(send_ref, side, groups))


def project(side, feat_t, w_inner, deg, send_lists, right_blocks, groups):
    hid = w_inner.shape[1]
    blocks, blk = deg.shape
    lists = send_lists.shape[0] // 2
    left_rows = (blocks - right_blocks) * blk
    return pl.pallas_call(
        functools.partial(project_kernel, groups=groups),
        in_specs=[SMEM, VMEM, VMEM, VMEM, VMEM],
        out_specs=[VMEM] * 3,
        out_shape=[
            jax.ShapeDtypeStruct((left_rows + lists, hid), jnp.bfloat16),
            jax.ShapeDtypeStruct((right_blocks * blk, hid), jnp.bfloat16),
            jax.ShapeDtypeStruct((blk, lists), jnp.int32),
        ],
        name="project",
    )(side, feat_t, w_inner, deg, send_lists)


def pick_rows(slots, table, first):
    chosen = one_hot_rows(slots - first, table.shape[0])
    return jnp.dot(chosen, table, preferred_element_type=jnp.float32)


def pick_near_kernel(left_ref, right_ref, slots_ref, out_ref):
    lists = out_ref.shape[0]
    left_rows = left_ref.shape[0] - lists
    for p in range(lists):
        column = slots_ref[:, p : p + 1]
        picked = pick_rows(column, left_ref[:left_rows], 0)
        picked = picked + pick_rows(column, right_ref[...], left_rows)
        out_ref[p] = picked.astype(out_ref.dtype)


def pick_near(left, right, slots):
    blk, lists = slots.shape
    return pl.pallas_call(
        pick_near_kernel,
        in_specs=[VMEM, VMEM, VMEM],
        out_specs=VMEM,
        out_shape=jax.ShapeDtypeStruct((lists, blk, left.shape[1]), jnp.bfloat16),
        name="pick_near",
    )(left, right, slots)


def pick_left_kernel(left_ref, out_ref, slots_ref):
    lists, blk, _ = out_ref.shape
    left_rows = left_ref.shape[0] - lists
    coded = left_ref[left_rows:].astype(jnp.float32)
    whole = coded[:, :blk] * 2.0**LIST_BITS + coded[:, blk : 2 * blk]
    slots = jnp.transpose(whole).astype(jnp.int32)
    slots_ref[...] = slots
    for p in range(lists):
        picked = pick_rows(slots[:, p : p + 1], left_ref[:left_rows], 0)
        out_ref[p] = picked.astype(out_ref.dtype)


def pick_left(left, lists, blk):
    return pl.pallas_call(
        pick_left_kernel,
        in_specs=[VMEM],
        out_specs=[VMEM, VMEM],
        out_shape=[
            jax.ShapeDtypeStruct((lists, blk, left.shape[1]), jnp.bfloat16),
            jax.ShapeDtypeStruct((blk, lists), jnp.int32),
        ],
        compiler_params=SMALL,
        name="pick_left",
    )(left)


def pick_right_kernel(part_ref, slots_ref, right_ref, out_ref, *, left_rows):
    for p in range(out_ref.shape[0]):
        picked = pick_rows(slots_ref[:, p : p + 1], right_ref[...], left_rows)
        out_ref[p] = (part_ref[p].astype(jnp.float32) + picked).astype(out_ref.dtype)


def pick_right(part, slots, right, left_rows):
    return pl.pallas_call(
        functools.partial(pick_right_kernel, left_rows=left_rows),
        in_specs=[VMEM, VMEM, VMEM],
        out_specs=VMEM,
        out_shape=jax.ShapeDtypeStruct(part.shape, part.dtype),
        compiler_params=SMALL,
        name="pick_right",
    )(part, slots, right)


def start_fetches(column_copies, tiles, tiles_v, sems):
    row_blocks = tiles.shape[0]
    firsts = [
        pltpu.make_async_copy(src, dst, sems.at[row_blocks + i])
        for i, (src, dst) in enumerate(column_copies)
    ]
    sets = [
        pltpu.make_async_copy(tiles.at[r], tiles_v.at[r], sems.at[r]) for r in range(row_blocks)
    ]
    for copy in firsts + sets:
        copy.start()

    def wait_columns():
        for copy in firsts:
            copy.wait()

    def wait_pair(first):
        for copy in sets[first : first + 2]:
            copy.wait()

    return wait_columns, wait_pair


def row_block_sum(tiles_v, columns, col_ref, r, product):
    total = None
    for t in range(0, tiles_v.shape[1], 2):
        left = jnp.concatenate([tiles_v[r, t], tiles_v[r, t + 1]], axis=1)
        part = product(left, columns[col_ref[r, t]], columns[col_ref[r, t + 1]])
        total = part if total is None else total + part
    return total


def row_blocks_in_pairs(row_blocks, wait_pair, block_sum, finish):
    ready = []
    for first in range(0, row_blocks, 2):
        wait_pair(first)
        sums = [(r, block_sum(r)) for r in range(first, min(first + 2, row_blocks))]
        for done in ready:
            finish(*done)
        ready = sums
    for done in ready:
        finish(*done)


def inner_kernel(
    col_ref, side_ref, left, right, near, far, tiles, deg_ref, bias_ref, wt_ref,
    send_ref, scores_ref, out_ref, columns, tiles_v, table, sems, *, groups,
):
    row_blocks, _, blk, _ = tiles.shape
    peers = send_ref.shape[0]
    rows = row_blocks * blk
    run = near.shape[0] // groups
    side = side_ref[0]
    right_blocks = right.shape[0] // blk
    copies = []
    for b in range(row_blocks):
        late = b - (row_blocks - right_blocks)
        source, at = (left, b) if late < 0 else (right, late)
        copies.append((source.at[pl.ds(at * blk, blk)], columns.at[b]))
    for g in range(groups):
        base = row_blocks + 2 * g * run
        group = pl.ds(g * run, run)
        copies.append((near.at[group], columns.at[pl.ds(base + side * run, run)]))
        copies.append((far.at[group], columns.at[pl.ds(base + (1 - side) * run, run)]))
    wait_columns, wait_pair = start_fetches(copies, tiles, tiles_v, sems)
    inv = inv_sqrt_columns(deg_ref)

    def finish(r, total):
        scale = inv[:, r : r + 1]
        hidden = (scale * jax.nn.relu(scale * total + bias_ref[...])).astype(jnp.bfloat16)
        scores = lax.dot_general(wt_ref[...], hidden, NT, preferred_element_type=jnp.float32)
        scores = scores.astype(jnp.bfloat16)
        scores_ref[r] = scores
        table[:, r * blk : (r + 1) * blk] = scores

    def block_sum(r):
        return row_block_sum(
            tiles_v, columns, col_ref, r, lambda left, a, b: jnp.dot(
                left, jnp.concatenate([a, b], axis=0), preferred_element_type=jnp.float32
            )
        )

    wait_columns()
    row_blocks_in_pairs(row_blocks, wait_pair, block_sum, finish)

    def pick(step, carry):
        base = step * 4
        for half in range(2):
            p = base + 2 * half
            slots = jnp.concatenate([send_ref[pl.ds(p, 1)], send_ref[pl.ds(p + 1, 1)]], axis=1)
            picked = jnp.dot(
                table[...], one_hot_cols(slots, rows), preferred_element_type=jnp.float32
            ).astype(out_ref.dtype)
            out_ref[p] = picked[:, :blk]
            out_ref[p + 1] = picked[:, blk:]
        return carry

    lax.fori_loop(0, peers // 4, pick, 0)


def aggregate_inner(
    tile_col, side, left, right, near, far, tiles, deg, bias, w_t, send_lists, groups
):
    classes, hid = w_t.shape
    blocks, blk = deg.shape
    peers = send_lists.shape[0]
    return pl.pallas_call(
        functools.partial(inner_kernel, groups=groups),
        in_specs=[SMEM, SMEM] + [ANY] * 4 + [HBM] + [VMEM] * 4,
        out_specs=[VMEM, VMEM],
        out_shape=[
            jax.ShapeDtypeStruct((blocks, classes, blk), jnp.bfloat16),
            jax.ShapeDtypeStruct((peers, classes, blk), jnp.bfloat16),
        ],
        scratch_shapes=[
            pltpu.VMEM((blocks + peers, blk, hid), jnp.bfloat16),
            pltpu.VMEM(tiles.shape, jnp.bfloat16),
            pltpu.VMEM((classes, blocks * blk), jnp.bfloat16),
            pltpu.SemaphoreType.DMA((2 * blocks + 2 * groups,)),
        ],
        compiler_params=ROOMY,
        name="aggregate_inner",
    )(tile_col, side, left, right, near, far, tiles, deg, bias, w_t, send_lists)


def outer_kernel(
    col_ref, own, arrived, tiles, deg_ref, bias_ref, out_ref, columns, tiles_v, sems
):
    row_blocks, _, blk, _ = tiles.shape
    classes = out_ref.shape[0]
    own_blocks = own.shape[0]
    copies = [
        (own, columns.at[pl.ds(0, own_blocks)]),
        (arrived, columns.at[pl.ds(own_blocks, arrived.shape[0])]),
    ]
    wait_columns, wait_pair = start_fetches(copies, tiles, tiles_v, sems)
    inv = lax.rsqrt(deg_ref[...].astype(jnp.float32))
    square = (classes, classes)
    diagonal = lax.broadcasted_iota(jnp.int32, square, 0) == lax.broadcasted_iota(jnp.int32, square, 1)
    bias = jnp.sum(jnp.where(diagonal, bias_ref[...], 0.0), axis=1, keepdims=True)

    def block_sum(r):
        return row_block_sum(
            tiles_v, columns, col_ref, r, lambda left, a, b: lax.dot_general(
                left, jnp.concatenate([a, b], axis=1), NT, preferred_element_type=jnp.float32
            )
        )

    def finish(r, total):
        out_ref[:, r * blk : (r + 1) * blk] = inv[r : r + 1] * jnp.transpose(total) + bias

    wait_columns()
    row_blocks_in_pairs(row_blocks, wait_pair, block_sum, finish)


def aggregate_outer(tile_col, own, arrived, tiles, deg, bias):
    blocks, classes, blk = own.shape
    peers = arrived.shape[0]
    return pl.pallas_call(
        outer_kernel,
        in_specs=[SMEM, ANY, ANY, HBM, VMEM, VMEM],
        out_specs=VMEM,
        out_shape=jax.ShapeDtypeStruct((classes, blocks * blk), jnp.float32),
        scratch_shapes=[
            pltpu.VMEM((blocks + peers, classes, blk), jnp.bfloat16),
            pltpu.VMEM(tiles.shape, jnp.bfloat16),
            pltpu.SemaphoreType.DMA((2 + blocks,)),
        ],
        compiler_params=ROOMY,
        name="aggregate_outer",
    )(tile_col, own, arrived, tiles, deg, bias)


def exchange(outgoing, axes):
    return lax.all_to_all(outgoing, axes, split_axis=0, concat_axis=0, tiled=True)


def mirror(block):
    return lax.ppermute(block, "hi", [(0, 1), (1, 0)])


def on_device(
    features, w_inner, bias_inner, w_outer, bias_outer, tiles, tile_col, degrees, send_rows, *, groups
):
    near_axes, all_axes = ("dom", "lo"), ("dom", "hi", "lo")
    send_lists = send_rows[0]
    blk = send_lists.shape[1]
    deg = degrees.reshape(-1, blk)
    side = lax.axis_index("hi").reshape(1)
    left, right, near_slots = project(side, features.T, w_inner, deg, send_lists, RIGHT_BLOCKS, groups)
    their_left = mirror(left)
    near_out = pick_near(left, right, near_slots)
    near = exchange(near_out, near_axes)
    their_right = mirror(right)
    part, slots = pick_left(their_left, send_lists.shape[0] // 2, blk)
    far_out = pick_right(part, slots, their_right, deg.size - right.shape[0])
    far = exchange(far_out, near_axes)
    own_scores, outgoing = aggregate_inner(
        tile_col, side, left, right, near, far, tiles, deg,
        bias_inner[None], w_outer.T, send_lists, groups,
    )
    arrived = exchange(outgoing, all_axes)
    return aggregate_outer(tile_col, own_scores, arrived, tiles, deg, bias_outer[None]).T


def solution(mesh):
    groups, inner = mesh.devices.shape
    halves = Mesh(mesh.devices.reshape(groups, 2, inner // 2), ("dom", "hi", "lo"))
    axes = ("dom", "hi", "lo")
    return jax.shard_map(
        functools.partial(on_device, groups=groups),
        mesh=halves,
        in_specs=(
            P(axes, None),
            P(),
            P(),
            P(),
            P(),
            P(axes, None, None, None),
            P(axes, None),
            P(axes),
            P(axes, None, None),
        ),
        out_specs=P(axes, None),
        check_vma=False,
    )
```

time: 95.2 us -> 94.5 us (level)
  blocking collectives: 72.1 us -> 39.7 us
  waiting for transfers between devices: 0 us -> 21.5 us
  starting transfers between devices: 0 us -> 8.63 us
  Pallas kernels: 22.7 us -> 24.1 us
    all_to_all x2, blocking collectives: 72.1 us -> 39.7 us  [exchange(): lax.all_to_all(outgoing, axes, split_axis=0, concat_axis=0, tiled=True)]
    ppermute x0 -> x2, waiting for transfers between devices: none -> 21.5 us  [mirror(): return lax.ppermute(block, 'hi', [(0, 1), (1, 0)])]
    all_to_all x0 -> x1, starting transfers between devices: none -> 6.24 us  [exchange(): lax.all_to_all(outgoing, axes, split_axis=0, concat_axis=0, tiled=True)]
    ppermute x0 -> x2, starting transfers between devices: none -> 2.38 us  [mirror(): return lax.ppermute(block, 'hi', [(0, 1), (1, 0)])]
    pallas_call x3 -> x6, Pallas kernels: 22.7 us -> 24.1 us  [the longest x1 9.79 us: aggregate_inner(): pl.pallas_call(functools.partial(inner_kernel, groups=groups), in_specs=[...]
  transfers between devices with their start and end apart: 0 -> 3, of which waited for: 0 -> 1; matrix products, arithmetic and copies ran while one was open for 0% -> 0% of each run, Pallas kernels for 0% -> 2%
where the time goes in v3:
time: 94.5 us; the launch traced here: 94.1 us
  blocking collectives  39.7 us (42%)
  Pallas kernels  24.1 us (26%)
  waiting for transfers between devices  21.5 us (23%)
  starting transfers between devices  8.63 us (9%)
    all_to_all x2, blocking collectives, exchange(): lax.all_to_all(outgoing, axes, split_axis=0, concat_axis=0, tiled=True)  39.7 us
    ppermute x2, waiting for transfers between devices, mirror(): return lax.ppermute(block, 'hi', [(0, 1), (1, 0)])  21.5 us
    pallas_call x1, Pallas kernels, aggregate_inner(): pl.pallas_call(functools.partial(inner_kernel, groups=groups), in_specs=[...  9.79 us
    all_to_all x1, starting transfers between devices, exchange(): lax.all_to_all(outgoing, axes, split_axis=0, concat_axis=0, tiled=True)  6.24 us
    pallas_call x1, Pallas kernels, aggregate_outer(): pl.pallas_call(outer_kernel, in_specs=[SMEM, ANY, ANY, HBM, VMEM, VMEM],...  6.02 us
    pallas_call x1, Pallas kernels, pick_near(): pl.pallas_call(pick_near_kernel, in_specs=[VMEM, VMEM, VMEM], out_specs=V...  3.6 us
    pallas_call x1, Pallas kernels, project(): pl.pallas_call(functools.partial(project_kernel, groups=groups), in_specs...  2.82 us
    ppermute x2, starting transfers between devices, mirror(): return lax.ppermute(block, 'hi', [(0, 1), (1, 0)])  2.38 us
  transfers between devices with their start and end apart: 3, of which 1 were waited for; matrix products, arithmetic and copies ran while one was open for 0% of the time, Pallas kernels for 2%

profile of v3, /device:TPU:1, one launch (start us, length us, event | category | flops | bytes accessed | tf_op | source)
XLA Modules:
  0.0 94.1 jit_solution(17699742386012930053)
XLA Ops:
  0.0 2.8 %project.1 = (bf16[400,256]{1,0:T(8,128)(2,1)}, bf16[640,256]{1,0:T(8,128)(2,1)}, s32[128,16]{1,0:T(8,128)}) custom-call(s32[1]{0:T(128)} %bitcast.side_ref, bf16[602,1024]{1,0:T(8,128)(2,1)} %bitcast.8, bf16[602,256]{1,0:T(8,128)(2,1)} %w_ref.1, s32[8,128]{1,0:T(8,128)} %bitcast.11, s32[32,128]{1,0:T(8,128)} %bitcast.9), custom_call_target="tpu_custom_call" | custom-call | tf_op jit(solution)/shard_map/project/pallas_call | solution.py:77
  2.8 3.6 %pick_near.1 = bf16[16,128,256]{2,1,0:T(8,128)(2,1)} custom-call(bf16[400,256]{1,0:T(8,128)(2,1)} %get-tuple-element.12.left_ref.left, bf16[640,256]{1,0:T(8,128)(2,1)} %get-tuple-element.13.right_ref.right, s32[128,16]{1,0:T(8,128)} %get-tuple-element.14.slots_ref), custom_call_target="tpu_custom_call" | custom-call | tf_op jit(solution)/shard_map/pick_near/pallas_call | solution.py:107
  6.4 6.2 %all-to-all-start = ((bf16[16,128,256]{2,1,0:T(8,128)(2,1)}), bf16[16,128,256]{2,1,0:T(8,128)(2,1)S(1)}, u32[]{:S(2)}, u32[]{:S(2)}) async-start(bf16[16,128,256]{2,1,0:T(8,128)(2,1)} %pick_near.1), calls=%async_computation | async-start | bytes 2097152 | tf_op jit(solution)/shard_map/all_to_all | solution.py:333
  12.7 2.3 %collective-permute-start.1 = (bf16[640,256]{1,0:T(8,128)(2,1)}, bf16[640,256]{1,0:T(8,128)(2,1)S(1)}, u32[]{:S(2)}, u32[]{:S(2)}) collective-permute-start(bf16[640,256]{1,0:T(8,128)(2,1)} %get-tuple-element.13.right_ref.right), channel_id=1, source_target_pairs={{0,2},{2,0},{1,3},{3,1},{4,6},{6,4},{5,7},{7,5},{8,10},{10,8},{9,1... | collective-permute-start | bytes 983048 | tf_op jit(solution)/shard_map/ppermute | solution.py:337
  15.0 0.1 collective-permute-start
  15.0 21.5 %collective-permute-done.left_ref = bf16[400,256]{1,0:T(8,128)(2,1)S(1)} collective-permute-done((bf16[400,256]{1,0:T(8,128)(2,1)}, bf16[400,256]{1,0:T(8,128)(2,1)S(1)}, u32[]{:S(2)}, u32[]{:S(2)}) %collective-permute-start) | collective-permute-done | bytes 204832 | tf_op jit(solution)/shard_map/ppermute | solution.py:337
  36.6 0.9 pick_left.1
  37.4 0.0 collective-permute-done.1.right_ref
  37.5 1.1 %pick_right.1 = bf16[16,128,256]{2,1,0:T(8,128)(2,1)S(1)} custom-call(bf16[16,128,256]{2,1,0:T(8,128)(2,1)S(1)} %get-tuple-element.15.part_ref, s32[128,16]{1,0:T(8,128)S(1)} %get-tuple-element.16.slots_ref, bf16[640,256]{1,0:T(8,128)(2,1)S(1)} %collective-permute-done.1.right_ref), custom_call_target="tpu_custom_call" | custom-call | tf_op jit(solution)/shard_map/pick_right/pallas_call | solution.py:149
  38.5 0.0 all-to-all-done.near
  38.5 0.0 copy-start
  38.5 21.8 %all_to_all.15.far = bf16[16,128,256]{2,1,0:T(8,128)(2,1)} all-to-all(bf16[16,128,256]{2,1,0:T(8,128)(2,1)S(1)} %pick_right.1), channel_id=1, replica_groups=mesh['dom'=8,'hi'=2,'lo'=2] {'dom','lo'}, dimensions={0} | all-to-all | bytes 2097152 | tf_op jit(solution)/shard_map/all_to_all | solution.py:333
  60.3 0.0 copy-done
  60.3 9.8 %aggregate_inner.1 = (bf16[8,41,128]{2,1,0:T(8,128)(2,1)}, bf16[32,41,128]{2,1,0:T(8,128)(2,1)}) custom-call(s32[8,32]{1,0:T(8,128)} %col_ref.3, s32[1]{0:T(128)} %bitcast.side_ref, bf16[400,256]{1,0:T(8,128)(2,1)} %get-tuple-element.12.left_ref.left, bf16[640,256]{1,0:T(8,128)(2,1)} %get-tuple-element.13.right_ref.right, bf16[16,128,256]{2,1,0:T(8,128)(2,1)} %copy-done, ...), custom_call_target="tpu_custom_call" | custom-call | tf_op jit(solution)/shard_map/aggregate_inner/pallas_call | solution.py:265
  70.1 17.9 %all_to_all.16.arrived = bf16[32,41,128]{2,1,0:T(8,128)(2,1)} all-to-all(bf16[32,41,128]{2,1,0:T(8,128)(2,1)} %get-tuple-element.18), channel_id=1, replica_groups=mesh['dom'=8,'hi'=2,'lo'=2] {'dom','hi','lo'}, dimensions={0} | all-to-all | bytes 671744 | tf_op jit(solution)/shard_map/all_to_all | solution.py:333
  88.1 6.0 %aggregate_outer.1 = f32[41,1024]{1,0:T(8,128)} custom-call(s32[8,32]{1,0:T(8,128)} %col_ref.3, bf16[8,41,128]{2,1,0:T(8,128)(2,1)} %get-tuple-element.17.own, bf16[32,41,128]{2,1,0:T(8,128)(2,1)} %all_to_all.16.arrived, bf16[8,32,128,128]{3,2,1,0:T(8,128)(2,1)} %tiles.3, s32[8,128]{1,0:T(8,128)} %bitcast.13, f32[1,41]{1,0:T(1,128)} %bitcast.16), custom_call_target="tpu_custom_call" | custom-call | tf_op jit(solution)/shard_map/aggregate_outer/pallas_call | solution.py:317
Async XLA Ops:
  6.4 32.1 %all-to-all-start = ((bf16[16,128,256]{2,1,0:T(8,128)(2,1)}), bf16[16,128,256]{2,1,0:T(8,128)(2,1)S(1)}, u32[]{:S(2)}, u32[]{:S(2)}) async-start(bf16[16,128,256]{2,1,0:T(8,128)(2,1)} %pick_near.1), calls=%async_computation | async-start | bytes 2097152 | tf_op jit(solution)/shard_map/all_to_all | solution.py:333
  12.7 24.8 %collective-permute-start.1 = (bf16[640,256]{1,0:T(8,128)(2,1)}, bf16[640,256]{1,0:T(8,128)(2,1)S(1)}, u32[]{:S(2)}, u32[]{:S(2)}) collective-permute-start(bf16[640,256]{1,0:T(8,128)(2,1)} %get-tuple-element.13.right_ref.right), channel_id=1, source_target_pairs={{0,2},{2,0},{1,3},{3,1},{4,6},{6,4},{5,7},{7,5},{8,10},{10,8},{9,1... | collective-permute-start | bytes 983048 | tf_op jit(solution)/shard_map/ppermute | solution.py:337
  15.0 21.6 %collective-permute-start = (bf16[400,256]{1,0:T(8,128)(2,1)}, bf16[400,256]{1,0:T(8,128)(2,1)S(1)}, u32[]{:S(2)}, u32[]{:S(2)}) collective-permute-start(bf16[400,256]{1,0:T(8,128)(2,1)} %get-tuple-element.12.left_ref.left), channel_id=1, source_target_pairs={{0,2},{2,0},{1,3},{3,1},{4,6},{6,4},{5,7},{7,5},{8,10},{10,8},{9,1... | collective-permute-start | bytes 614408 | tf_op jit(solution)/shard_map/ppermute | solution.py:337
  38.5 21.8 %copy-start = (bf16[16,128,256]{2,1,0:T(8,128)(2,1)}, bf16[16,128,256]{2,1,0:T(8,128)(2,1)S(1)}, u32[]{:S(2)}) copy-start(bf16[16,128,256]{2,1,0:T(8,128)(2,1)S(1)} %all-to-all-done.near) | copy-start | bytes 3145732

commit v4 on v3

--- a/solution.py
+++ b/solution.py
@@ -79,9 +79,9 @@
         in_specs=[SMEM, VMEM, VMEM, VMEM, VMEM],
         out_specs=[VMEM] * 3,
         out_shape=[
-            jax.ShapeDtypeStruct((left_rows + lists, hid), jnp.bfloat16),
-            jax.ShapeDtypeStruct((right_blocks * blk, hid), jnp.bfloat16),
-            jax.ShapeDtypeStruct((blk, lists), jnp.int32),
+            pltpu.VMEM((left_rows + lists, hid), jnp.bfloat16),
+            pltpu.VMEM((right_blocks * blk, hid), jnp.bfloat16),
+            pltpu.VMEM((blk, lists), jnp.int32),
         ],
         name="project",
     )(side, feat_t, w_inner, deg, send_lists)
@@ -108,7 +108,8 @@
         pick_near_kernel,
         in_specs=[VMEM, VMEM, VMEM],
         out_specs=VMEM,
-        out_shape=jax.ShapeDtypeStruct((lists, blk, left.shape[1]), jnp.bfloat16),
+        out_shape=pltpu.VMEM((lists, blk, left.shape[1]), jnp.bfloat16),
+        compiler_params=SMALL,
         name="pick_near",
     )(left, right, slots)
 
@@ -131,8 +132,8 @@
         in_specs=[VMEM],
         out_specs=[VMEM, VMEM],
         out_shape=[
-            jax.ShapeDtypeStruct((lists, blk, left.shape[1]), jnp.bfloat16),
-            jax.ShapeDtypeStruct((blk, lists), jnp.int32),
+            pltpu.VMEM((lists, blk, left.shape[1]), jnp.bfloat16),
+            pltpu.VMEM((blk, lists), jnp.int32),
         ],
         compiler_params=SMALL,
         name="pick_left",
@@ -150,7 +151,7 @@
         functools.partial(pick_right_kernel, left_rows=left_rows),
         in_specs=[VMEM, VMEM, VMEM],
         out_specs=VMEM,
-        out_shape=jax.ShapeDtypeStruct(part.shape, part.dtype),
+        out_shape=pltpu.VMEM(part.shape, part.dtype),
         compiler_params=SMALL,
         name="pick_right",
     )(part, slots, right)
@@ -188,11 +189,11 @@
     return total
 
 
-def row_blocks_in_pairs(row_blocks, wait_pair, block_sum, finish):
+def row_blocks_in_pairs(row_blocks, wait_pair, pair_sums, finish):
     ready = []
     for first in range(0, row_blocks, 2):
         wait_pair(first)
-        sums = [(r, block_sum(r)) for r in range(first, min(first + 2, row_blocks))]
+        sums = pair_sums(first)
         for done in ready:
             finish(*done)
         ready = sums
@@ -231,15 +232,16 @@
         scores_ref[r] = scores
         table[:, r * blk : (r + 1) * blk] = scores
 
-    def block_sum(r):
-        return row_block_sum(
-            tiles_v, columns, col_ref, r, lambda left, a, b: jnp.dot(
-                left, jnp.concatenate([a, b], axis=0), preferred_element_type=jnp.float32
-            )
-        )
+    def pair_sums(first):
+        def product(left, a, b):
+            right = jnp.concatenate([a, b], axis=0)
+            return jnp.dot(left, right, preferred_element_type=jnp.float32)
+
+        pair = range(first, min(first + 2, row_blocks))
+        return [(r, row_block_sum(tiles_v, columns, col_ref, r, product)) for r in pair]
 
     wait_columns()
-    row_blocks_in_pairs(row_blocks, wait_pair, block_sum, finish)
+    row_blocks_in_pairs(row_blocks, wait_pair, pair_sums, finish)
 
     def pick(step, carry):
         base = step * 4
@@ -267,8 +269,8 @@
         in_specs=[SMEM, SMEM] + [ANY] * 4 + [HBM] + [VMEM] * 4,
         out_specs=[VMEM, VMEM],
         out_shape=[
-            jax.ShapeDtypeStruct((blocks, classes, blk), jnp.bfloat16),
-            jax.ShapeDtypeStruct((peers, classes, blk), jnp.bfloat16),
+            pltpu.VMEM((blocks, classes, blk), jnp.bfloat16),
+            pltpu.VMEM((peers, classes, blk), jnp.bfloat16),
         ],
         scratch_shapes=[
             pltpu.VMEM((blocks + peers, blk, hid), jnp.bfloat16),
@@ -284,7 +286,7 @@
 def outer_kernel(
     col_ref, own, arrived, tiles, deg_ref, bias_ref, out_ref, columns, tiles_v, sems
 ):
-    row_blocks, _, blk, _ = tiles.shape
+    row_blocks, per_row, blk, _ = tiles.shape
     classes = out_ref.shape[0]
     own_blocks = own.shape[0]
     copies = [
@@ -297,18 +299,30 @@
     diagonal = lax.broadcasted_iota(jnp.int32, square, 0) == lax.broadcasted_iota(jnp.int32, square, 1)
     bias = jnp.sum(jnp.where(diagonal, bias_ref[...], 0.0), axis=1, keepdims=True)
 
-    def block_sum(r):
-        return row_block_sum(
-            tiles_v, columns, col_ref, r, lambda left, a, b: lax.dot_general(
-                left, jnp.concatenate([a, b], axis=1), NT, preferred_element_type=jnp.float32
-            )
-        )
-
-    def finish(r, total):
-        out_ref[:, r * blk : (r + 1) * blk] = inv[r : r + 1] * jnp.transpose(total) + bias
+    def pair_sums(first):
+        pair = range(first, min(first + 2, row_blocks))
+        sums = {r: [None, None] for r in pair}
+        for t in range(0, per_row, 4):
+            for form in range(2):
+                for r in pair:
+                    kind = (form + r) % 2
+                    u = t + 2 * kind
+                    tile = jnp.concatenate([tiles_v[r, u], tiles_v[r, u + 1]], axis=1)
+                    block = jnp.concatenate(
+                        [columns[col_ref[r, u]], columns[col_ref[r, u + 1]]], axis=1
+                    )
+                    operands = (block, tile) if kind else (tile, block)
+                    part = lax.dot_general(*operands, NT, preferred_element_type=jnp.float32)
+                    known = sums[r][kind]
+                    sums[r][kind] = part if known is None else known + part
+        return list(sums.items())
+
+    def finish(r, sums):
+        total = jnp.transpose(sums[0]) + sums[1]
+        out_ref[:, r * blk : (r + 1) * blk] = inv[r : r + 1] * total + bias
 
     wait_columns()
-    row_blocks_in_pairs(row_blocks, wait_pair, block_sum, finish)
+    row_blocks_in_pairs(row_blocks, wait_pair, pair_sums, finish)
 
 
 def aggregate_outer(tile_col, own, arrived, tiles, deg, bias):

time: 94.5 us -> 91.3 us (0.966)
  Pallas kernels: 24.1 us -> 21.3 us
    pallas_call x1, Pallas kernels: 3.6 us -> 2.57 us  [pick_near(): pl.pallas_call(pick_near_kernel, in_specs=[VMEM, VMEM, VMEM], out_specs=V...]
where the time goes in v4:
time: 91.3 us; the launch traced here: 90.9 us
  blocking collectives  39.4 us (43%)
  waiting for transfers between devices  21.4 us (23%)
  Pallas kernels  21.3 us (23%)
  starting transfers between devices  8.62 us (9%)
    all_to_all x2, blocking collectives, exchange(): lax.all_to_all(outgoing, axes, split_axis=0, concat_axis=0, tiled=True)  39.4 us
    ppermute x2, waiting for transfers between devices, mirror(): return lax.ppermute(block, 'hi', [(0, 1), (1, 0)])  21.4 us
    pallas_call x1, Pallas kernels, aggregate_inner(): pl.pallas_call(functools.partial(inner_kernel, groups=groups), in_specs=[...  9.06 us
    all_to_all x1, starting transfers between devices, exchange(): lax.all_to_all(outgoing, axes, split_axis=0, concat_axis=0, tiled=True)  6.24 us
    pallas_call x1, Pallas kernels, aggregate_outer(): pl.pallas_call(outer_kernel, in_specs=[SMEM, ANY, ANY, HBM, VMEM, VMEM],...  5.67 us
    pallas_call x1, Pallas kernels, pick_near(): pl.pallas_call(pick_near_kernel, in_specs=[VMEM, VMEM, VMEM], out_specs=V...  2.57 us
    ppermute x2, starting transfers between devices, mirror(): return lax.ppermute(block, 'hi', [(0, 1), (1, 0)])  2.38 us
    pallas_call x1, Pallas kernels, project(): pl.pallas_call(functools.partial(project_kernel, groups=groups), in_specs...  2.08 us
  transfers between devices with their start and end apart: 3, of which 1 were waited for; matrix products, arithmetic and copies ran while one was open for 0% of the time, Pallas kernels for 2%

profile of v4, /device:TPU:1, one launch (start us, length us, event | category | flops | bytes accessed | tf_op | source)
XLA Modules:
  0.0 90.9 jit_solution(8317586574186547990)
XLA Ops:
  0.0 2.1 %project.1 = (bf16[400,256]{1,0:T(8,128)(2,1)S(1)}, bf16[640,256]{1,0:T(8,128)(2,1)S(1)}, s32[128,16]{1,0:T(8,128)S(1)}) custom-call(s32[1]{0:T(128)} %bitcast.side_ref, bf16[602,1024]{1,0:T(8,128)(2,1)} %bitcast.8, bf16[602,256]{1,0:T(8,128)(2,1)} %w_ref.1, s32[8,128]{1,0:T(8,128)} %bitcast.11, s32[32,128]{1,0:T(8,128)} %bitcast.9), custom_call_target="tpu_custom_call" | custom-call | tf_op jit(solution)/shard_map/project/pallas_call | solution.py:77
  2.1 0.0 copy-start
  2.1 0.0 copy-start.1
  2.1 2.6 %pick_near.1 = bf16[16,128,256]{2,1,0:T(8,128)(2,1)} custom-call(bf16[400,256]{1,0:T(8,128)(2,1)S(1)} %get-tuple-element.12.left_ref.left, bf16[640,256]{1,0:T(8,128)(2,1)S(1)} %get-tuple-element.13.right_ref.right, s32[128,16]{1,0:T(8,128)S(1)} %get-tuple-element.14.slots_ref), custom_call_target="tpu_custom_call" | custom-call | tf_op jit(solution)/shard_map/pick_near/pallas_call | solution.py:107
  4.7 6.2 %all-to-all-start = ((bf16[16,128,256]{2,1,0:T(8,128)(2,1)}), bf16[16,128,256]{2,1,0:T(8,128)(2,1)S(1)}, u32[]{:S(2)}, u32[]{:S(2)}) async-start(bf16[16,128,256]{2,1,0:T(8,128)(2,1)} %pick_near.1), calls=%async_computation | async-start | bytes 2097152 | tf_op jit(solution)/shard_map/all_to_all | solution.py:347
  10.9 2.3 %collective-permute-start.1 = (bf16[640,256]{1,0:T(8,128)(2,1)S(1)}, bf16[640,256]{1,0:T(8,128)(2,1)S(1)}, u32[]{:S(2)}, u32[]{:S(2)}) collective-permute-start(bf16[640,256]{1,0:T(8,128)(2,1)S(1)} %get-tuple-element.13.right_ref.right), channel_id=1, source_target_pairs={{0,2},{2,0},{1,3},{3,1},{4,6},{6,4},{5,7},{7,5},{8,10},{10,8},{9,1... | collective-permute-start | bytes 983048 | tf_op jit(solution)/shard_map/ppermute | solution.py:351
  13.2 0.1 collective-permute-start
  13.3 21.4 %collective-permute-done.left_ref = bf16[400,256]{1,0:T(8,128)(2,1)S(1)} collective-permute-done((bf16[400,256]{1,0:T(8,128)(2,1)S(1)}, bf16[400,256]{1,0:T(8,128)(2,1)S(1)}, u32[]{:S(2)}, u32[]{:S(2)}) %collective-permute-start) | collective-permute-done | bytes 204832 | tf_op jit(solution)/shard_map/ppermute | solution.py:351
  34.7 0.9 pick_left.1
  35.6 0.0 collective-permute-done.1.right_ref
  35.6 1.1 %pick_right.1 = bf16[16,128,256]{2,1,0:T(8,128)(2,1)S(1)} custom-call(bf16[16,128,256]{2,1,0:T(8,128)(2,1)S(1)} %get-tuple-element.15.part_ref, s32[128,16]{1,0:T(8,128)S(1)} %get-tuple-element.16.slots_ref, bf16[640,256]{1,0:T(8,128)(2,1)S(1)} %collective-permute-done.1.right_ref), custom_call_target="tpu_custom_call" | custom-call | tf_op jit(solution)/shard_map/pick_right/pallas_call | solution.py:150
  36.7 0.0 all-to-all-done.near
  36.7 0.0 copy-start.3
  36.7 21.9 %all_to_all.15.far = bf16[16,128,256]{2,1,0:T(8,128)(2,1)} all-to-all(bf16[16,128,256]{2,1,0:T(8,128)(2,1)S(1)} %pick_right.1), channel_id=1, replica_groups=mesh['dom'=8,'hi'=2,'lo'=2] {'dom','lo'}, dimensions={0} | all-to-all | bytes 2097152 | tf_op jit(solution)/shard_map/all_to_all | solution.py:347
  58.6 0.0 copy-done
  58.6 0.0 copy-done.1
  58.7 0.0 copy-done.3
  58.7 9.1 %aggregate_inner.1 = (bf16[8,41,128]{2,1,0:T(8,128)(2,1)S(1)}, bf16[32,41,128]{2,1,0:T(8,128)(2,1)S(1)}) custom-call(s32[8,32]{1,0:T(8,128)} %col_ref.3, s32[1]{0:T(128)} %bitcast.side_ref, bf16[400,256]{1,0:T(8,128)(2,1)} %copy-done.1, bf16[640,256]{1,0:T(8,128)(2,1)} %copy-done, bf16[16,128,256]{2,1,0:T(8,128)(2,1)} %copy-done.3, ...), custom_call_target="tpu_custom_call" | custom-call | tf_op jit(solution)/shard_map/aggregate_inner/pallas_call | solution.py:267
  67.7 0.0 copy-start.2
  67.7 17.5 %all_to_all.16.arrived = bf16[32,41,128]{2,1,0:T(8,128)(2,1)} all-to-all(bf16[32,41,128]{2,1,0:T(8,128)(2,1)S(1)} %get-tuple-element.18), channel_id=1, replica_groups=mesh['dom'=8,'hi'=2,'lo'=2] {'dom','hi','lo'}, dimensions={0} | all-to-all | bytes 671744 | tf_op jit(solution)/shard_map/all_to_all | solution.py:347
  85.2 0.0 copy-done.2
  85.2 5.7 %aggregate_outer.1 = f32[41,1024]{1,0:T(8,128)} custom-call(s32[8,32]{1,0:T(8,128)} %col_ref.3, bf16[8,41,128]{2,1,0:T(8,128)(2,1)} %copy-done.2, bf16[32,41,128]{2,1,0:T(8,128)(2,1)} %all_to_all.16.arrived, bf16[8,32,128,128]{3,2,1,0:T(8,128)(2,1)} %tiles.3, s32[8,128]{1,0:T(8,128)} %bitcast.13, f32[1,41]{1,0:T(1,128)} %bitcast.16), custom_call_target="tpu_custom_call" | custom-call | tf_op jit(solution)/shard_map/aggregate_outer/pallas_call | solution.py:331
Async XLA Ops:
  2.1 56.6 %copy-start = (bf16[640,256]{1,0:T(8,128)(2,1)}, bf16[640,256]{1,0:T(8,128)(2,1)S(1)}, u32[]{:S(2)}) copy-start(bf16[640,256]{1,0:T(8,128)(2,1)S(1)} %get-tuple-element.13.right_ref.right) | copy-start | bytes 983044
  2.1 56.6 %copy-start.1 = (bf16[400,256]{1,0:T(8,128)(2,1)}, bf16[400,256]{1,0:T(8,128)(2,1)S(1)}, u32[]{:S(2)}) copy-start(bf16[400,256]{1,0:T(8,128)(2,1)S(1)} %get-tuple-element.12.left_ref.left) | copy-start | bytes 614404
  4.7 32.0 %all-to-all-start = ((bf16[16,128,256]{2,1,0:T(8,128)(2,1)}), bf16[16,128,256]{2,1,0:T(8,128)(2,1)S(1)}, u32[]{:S(2)}, u32[]{:S(2)}) async-start(bf16[16,128,256]{2,1,0:T(8,128)(2,1)} %pick_near.1), calls=%async_computation | async-start | bytes 2097152 | tf_op jit(solution)/shard_map/all_to_all | solution.py:347
  10.9 24.7 %collective-permute-start.1 = (bf16[640,256]{1,0:T(8,128)(2,1)S(1)}, bf16[640,256]{1,0:T(8,128)(2,1)S(1)}, u32[]{:S(2)}, u32[]{:S(2)}) collective-permute-start(bf16[640,256]{1,0:T(8,128)(2,1)S(1)} %get-tuple-element.13.right_ref.right), channel_id=1, source_target_pairs={{0,2},{2,0},{1,3},{3,1},{4,6},{6,4},{5,7},{7,5},{8,10},{10,8},{9,1... | collective-permute-start | bytes 983048 | tf_op jit(solution)/shard_map/ppermute | solution.py:351
  13.2 21.5 %collective-permute-start = (bf16[400,256]{1,0:T(8,128)(2,1)S(1)}, bf16[400,256]{1,0:T(8,128)(2,1)S(1)}, u32[]{:S(2)}, u32[]{:S(2)}) collective-permute-start(bf16[400,256]{1,0:T(8,128)(2,1)S(1)} %get-tuple-element.12.left_ref.left), channel_id=1, source_target_pairs={{0,2},{2,0},{1,3},{3,1},{4,6},{6,4},{5,7},{7,5},{8,10},{10,8},{9,1... | collective-permute-start | bytes 614408 | tf_op jit(solution)/shard_map/ppermute | solution.py:351
  36.7 21.9 %copy-start.3 = (bf16[16,128,256]{2,1,0:T(8,128)(2,1)}, bf16[16,128,256]{2,1,0:T(8,128)(2,1)S(1)}, u32[]{:S(2)}) copy-start(bf16[16,128,256]{2,1,0:T(8,128)(2,1)S(1)} %all-to-all-done.near) | copy-start | bytes 3145732
  67.7 17.5 %copy-start.2 = (bf16[8,41,128]{2,1,0:T(8,128)(2,1)}, bf16[8,41,128]{2,1,0:T(8,128)(2,1)S(1)}, u32[]{:S(2)}) copy-start(bf16[8,41,128]{2,1,0:T(8,128)(2,1)S(1)} %get-tuple-element.17.own) | copy-start | bytes 251908

commit v5 on v4

--- a/solution.py
+++ b/solution.py
@@ -95,10 +95,9 @@
 def pick_near_kernel(left_ref, right_ref, slots_ref, out_ref):
     lists = out_ref.shape[0]
     left_rows = left_ref.shape[0] - lists
+    table = jnp.concatenate([left_ref[:left_rows], right_ref[...]], axis=0)
     for p in range(lists):
-        column = slots_ref[:, p : p + 1]
-        picked = pick_rows(column, left_ref[:left_rows], 0)
-        picked = picked + pick_rows(column, right_ref[...], left_rows)
+        picked = pick_rows(slots_ref[:, p : p + 1], table, 0)
         out_ref[p] = picked.astype(out_ref.dtype)
 
 
@@ -255,7 +254,7 @@
             out_ref[p + 1] = picked[:, blk:]
         return carry
 
-    lax.fori_loop(0, peers // 4, pick, 0)
+    lax.fori_loop(0, peers // 4, pick, 0, unroll=8)
 
 
 def aggregate_inner(

time: 91.3 us -> 90.1 us (0.987)
  Pallas kernels: 21.3 us -> 20.2 us
where the time goes in v5:
time: 90.1 us; the launch traced here: 89.7 us
  blocking collectives  39.4 us (44%)
  waiting for transfers between devices  21.4 us (24%)
  Pallas kernels  20.2 us (22%)
  starting transfers between devices  8.62 us (10%)
    all_to_all x2, blocking collectives, exchange(): lax.all_to_all(outgoing, axes, split_axis=0, concat_axis=0, tiled=True)  39.4 us
    ppermute x2, waiting for transfers between devices, mirror(): return lax.ppermute(block, 'hi', [(0, 1), (1, 0)])  21.4 us
    pallas_call x1, Pallas kernels, aggregate_inner(): pl.pallas_call(functools.partial(inner_kernel, groups=groups), in_specs=[...  8.2 us
    all_to_all x1, starting transfers between devices, exchange(): lax.all_to_all(outgoing, axes, split_axis=0, concat_axis=0, tiled=True)  6.23 us
    pallas_call x1, Pallas kernels, aggregate_outer(): pl.pallas_call(outer_kernel, in_specs=[SMEM, ANY, ANY, HBM, VMEM, VMEM],...  5.66 us
    ppermute x2, starting transfers between devices, mirror(): return lax.ppermute(block, 'hi', [(0, 1), (1, 0)])  2.38 us
    pallas_call x1, Pallas kernels, pick_near(): pl.pallas_call(pick_near_kernel, in_specs=[VMEM, VMEM, VMEM], out_specs=V...  2.29 us
    pallas_call x1, Pallas kernels, project(): pl.pallas_call(functools.partial(project_kernel, groups=groups), in_specs...  2.08 us
  transfers between devices with their start and end apart: 3, of which 1 were waited for; matrix products, arithmetic and copies ran while one was open for 0% of the time, Pallas kernels for 2%

profile of v5, /device:TPU:1, one launch (start us, length us, event | category | flops | bytes accessed | tf_op | source)
XLA Modules:
  0.0 89.7 jit_solution(11512197223752818194)
XLA Ops:
  0.0 2.1 %project.1 = (bf16[400,256]{1,0:T(8,128)(2,1)S(1)}, bf16[640,256]{1,0:T(8,128)(2,1)S(1)}, s32[128,16]{1,0:T(8,128)S(1)}) custom-call(s32[1]{0:T(128)} %bitcast.side_ref, bf16[602,1024]{1,0:T(8,128)(2,1)} %bitcast.8, bf16[602,256]{1,0:T(8,128)(2,1)} %w_ref.1, s32[8,128]{1,0:T(8,128)} %bitcast.11, s32[32,128]{1,0:T(8,128)} %bitcast.9), custom_call_target="tpu_custom_call" | custom-call | tf_op jit(solution)/shard_map/project/pallas_call | solution.py:77
  2.1 0.0 copy-start
  2.1 0.0 copy-start.1
  2.1 2.3 %pick_near.1 = bf16[16,128,256]{2,1,0:T(8,128)(2,1)} custom-call(bf16[400,256]{1,0:T(8,128)(2,1)S(1)} %get-tuple-element.12.left_ref.left, bf16[640,256]{1,0:T(8,128)(2,1)S(1)} %get-tuple-element.13.right_ref.right, s32[128,16]{1,0:T(8,128)S(1)} %get-tuple-element.14.slots_ref), custom_call_target="tpu_custom_call" | custom-call | tf_op jit(solution)/shard_map/pick_near/pallas_call | solution.py:106
  4.4 6.2 %all-to-all-start = ((bf16[16,128,256]{2,1,0:T(8,128)(2,1)}), bf16[16,128,256]{2,1,0:T(8,128)(2,1)S(1)}, u32[]{:S(2)}, u32[]{:S(2)}) async-start(bf16[16,128,256]{2,1,0:T(8,128)(2,1)} %pick_near.1), calls=%async_computation | async-start | bytes 2097152 | tf_op jit(solution)/shard_map/all_to_all | solution.py:346
  10.6 2.3 %collective-permute-start.1 = (bf16[640,256]{1,0:T(8,128)(2,1)S(1)}, bf16[640,256]{1,0:T(8,128)(2,1)S(1)}, u32[]{:S(2)}, u32[]{:S(2)}) collective-permute-start(bf16[640,256]{1,0:T(8,128)(2,1)S(1)} %get-tuple-element.13.right_ref.right), channel_id=1, source_target_pairs={{0,2},{2,0},{1,3},{3,1},{4,6},{6,4},{5,7},{7,5},{8,10},{10,8},{9,1... | collective-permute-start | bytes 983048 | tf_op jit(solution)/shard_map/ppermute | solution.py:350
  12.9 0.1 collective-permute-start
  13.0 21.4 %collective-permute-done.left_ref = bf16[400,256]{1,0:T(8,128)(2,1)S(1)} collective-permute-done((bf16[400,256]{1,0:T(8,128)(2,1)S(1)}, bf16[400,256]{1,0:T(8,128)(2,1)S(1)}, u32[]{:S(2)}, u32[]{:S(2)}) %collective-permute-start) | collective-permute-done | bytes 204832 | tf_op jit(solution)/shard_map/ppermute | solution.py:350
  34.4 0.9 pick_left.1
  35.3 0.0 collective-permute-done.1.right_ref
  35.3 1.1 %pick_right.1 = bf16[16,128,256]{2,1,0:T(8,128)(2,1)S(1)} custom-call(bf16[16,128,256]{2,1,0:T(8,128)(2,1)S(1)} %get-tuple-element.15.part_ref, s32[128,16]{1,0:T(8,128)S(1)} %get-tuple-element.16.slots_ref, bf16[640,256]{1,0:T(8,128)(2,1)S(1)} %collective-permute-done.1.right_ref), custom_call_target="tpu_custom_call" | custom-call | tf_op jit(solution)/shard_map/pick_right/pallas_call | solution.py:149
  36.4 0.0 all-to-all-done.near
  36.4 0.0 copy-start.3
  36.5 21.9 %all_to_all.15.far = bf16[16,128,256]{2,1,0:T(8,128)(2,1)} all-to-all(bf16[16,128,256]{2,1,0:T(8,128)(2,1)S(1)} %pick_right.1), channel_id=1, replica_groups=mesh['dom'=8,'hi'=2,'lo'=2] {'dom','lo'}, dimensions={0} | all-to-all | bytes 2097152 | tf_op jit(solution)/shard_map/all_to_all | solution.py:346
  58.3 0.0 copy-done
  58.4 0.0 copy-done.1
  58.4 0.0 copy-done.3
  58.4 8.2 %aggregate_inner.1 = (bf16[8,41,128]{2,1,0:T(8,128)(2,1)S(1)}, bf16[32,41,128]{2,1,0:T(8,128)(2,1)S(1)}) custom-call(s32[8,32]{1,0:T(8,128)} %col_ref.3, s32[1]{0:T(128)} %bitcast.side_ref, bf16[400,256]{1,0:T(8,128)(2,1)} %copy-done.1, bf16[640,256]{1,0:T(8,128)(2,1)} %copy-done, bf16[16,128,256]{2,1,0:T(8,128)(2,1)} %copy-done.3, ...), custom_call_target="tpu_custom_call" | custom-call | tf_op jit(solution)/shard_map/aggregate_inner/pallas_call | solution.py:266
  66.6 0.0 copy-start.2
  66.6 17.5 %all_to_all.16.arrived = bf16[32,41,128]{2,1,0:T(8,128)(2,1)} all-to-all(bf16[32,41,128]{2,1,0:T(8,128)(2,1)S(1)} %get-tuple-element.18), channel_id=1, replica_groups=mesh['dom'=8,'hi'=2,'lo'=2] {'dom','hi','lo'}, dimensions={0} | all-to-all | bytes 671744 | tf_op jit(solution)/shard_map/all_to_all | solution.py:346
  84.1 0.0 copy-done.2
  84.1 5.7 %aggregate_outer.1 = f32[41,1024]{1,0:T(8,128)} custom-call(s32[8,32]{1,0:T(8,128)} %col_ref.3, bf16[8,41,128]{2,1,0:T(8,128)(2,1)} %copy-done.2, bf16[32,41,128]{2,1,0:T(8,128)(2,1)} %all_to_all.16.arrived, bf16[8,32,128,128]{3,2,1,0:T(8,128)(2,1)} %tiles.3, s32[8,128]{1,0:T(8,128)} %bitcast.13, f32[1,41]{1,0:T(1,128)} %bitcast.16), custom_call_target="tpu_custom_call" | custom-call | tf_op jit(solution)/shard_map/aggregate_outer/pallas_call | solution.py:330
Async XLA Ops:
  2.1 56.3 %copy-start = (bf16[640,256]{1,0:T(8,128)(2,1)}, bf16[640,256]{1,0:T(8,128)(2,1)S(1)}, u32[]{:S(2)}) copy-start(bf16[640,256]{1,0:T(8,128)(2,1)S(1)} %get-tuple-element.13.right_ref.right) | copy-start | bytes 983044
  2.1 56.3 %copy-start.1 = (bf16[400,256]{1,0:T(8,128)(2,1)}, bf16[400,256]{1,0:T(8,128)(2,1)S(1)}, u32[]{:S(2)}) copy-start(bf16[400,256]{1,0:T(8,128)(2,1)S(1)} %get-tuple-element.12.left_ref.left) | copy-start | bytes 614404
  4.4 32.0 %all-to-all-start = ((bf16[16,128,256]{2,1,0:T(8,128)(2,1)}), bf16[16,128,256]{2,1,0:T(8,128)(2,1)S(1)}, u32[]{:S(2)}, u32[]{:S(2)}) async-start(bf16[16,128,256]{2,1,0:T(8,128)(2,1)} %pick_near.1), calls=%async_computation | async-start | bytes 2097152 | tf_op jit(solution)/shard_map/all_to_all | solution.py:346
  10.6 24.7 %collective-permute-start.1 = (bf16[640,256]{1,0:T(8,128)(2,1)S(1)}, bf16[640,256]{1,0:T(8,128)(2,1)S(1)}, u32[]{:S(2)}, u32[]{:S(2)}) collective-permute-start(bf16[640,256]{1,0:T(8,128)(2,1)S(1)} %get-tuple-element.13.right_ref.right), channel_id=1, source_target_pairs={{0,2},{2,0},{1,3},{3,1},{4,6},{6,4},{5,7},{7,5},{8,10},{10,8},{9,1... | collective-permute-start | bytes 983048 | tf_op jit(solution)/shard_map/ppermute | solution.py:350
  12.9 21.5 %collective-permute-start = (bf16[400,256]{1,0:T(8,128)(2,1)S(1)}, bf16[400,256]{1,0:T(8,128)(2,1)S(1)}, u32[]{:S(2)}, u32[]{:S(2)}) collective-permute-start(bf16[400,256]{1,0:T(8,128)(2,1)S(1)} %get-tuple-element.12.left_ref.left), channel_id=1, source_target_pairs={{0,2},{2,0},{1,3},{3,1},{4,6},{6,4},{5,7},{7,5},{8,10},{10,8},{9,1... | collective-permute-start | bytes 614408 | tf_op jit(solution)/shard_map/ppermute | solution.py:350
  36.4 21.9 %copy-start.3 = (bf16[16,128,256]{2,1,0:T(8,128)(2,1)}, bf16[16,128,256]{2,1,0:T(8,128)(2,1)S(1)}, u32[]{:S(2)}) copy-start(bf16[16,128,256]{2,1,0:T(8,128)(2,1)S(1)} %all-to-all-done.near) | copy-start | bytes 3145732
  66.6 17.5 %copy-start.2 = (bf16[8,41,128]{2,1,0:T(8,128)(2,1)}, bf16[8,41,128]{2,1,0:T(8,128)(2,1)S(1)}, u32[]{:S(2)}) copy-start(bf16[8,41,128]{2,1,0:T(8,128)(2,1)S(1)} %get-tuple-element.17.own) | copy-start | bytes 251908

commit v6 on v5

--- a/solution.py
+++ b/solution.py
@@ -92,22 +92,33 @@
     return jnp.dot(chosen, table, preferred_element_type=jnp.float32)
 
 
-def pick_near_kernel(left_ref, right_ref, slots_ref, out_ref):
-    lists = out_ref.shape[0]
+def pick_near_kernel(left_ref, right_ref, slots_ref, out, picked_ref, sems):
+    lists = picked_ref.shape[0]
+    chunk = lists // sems.shape[0]
     left_rows = left_ref.shape[0] - lists
     table = jnp.concatenate([left_ref[:left_rows], right_ref[...]], axis=0)
+    copies = []
     for p in range(lists):
         picked = pick_rows(slots_ref[:, p : p + 1], table, 0)
-        out_ref[p] = picked.astype(out_ref.dtype)
+        picked_ref[p] = picked.astype(picked_ref.dtype)
+        if (p + 1) % chunk == 0:
+            part = pl.ds(p + 1 - chunk, chunk)
+            copy = pltpu.make_async_copy(picked_ref.at[part], out.at[part], sems.at[p // chunk])
+            copy.start()
+            copies.append(copy)
+    for copy in copies:
+        copy.wait()
 
 
 def pick_near(left, right, slots):
     blk, lists = slots.shape
+    shape = (lists, blk, left.shape[1])
     return pl.pallas_call(
         pick_near_kernel,
         in_specs=[VMEM, VMEM, VMEM],
-        out_specs=VMEM,
-        out_shape=pltpu.VMEM((lists, blk, left.shape[1]), jnp.bfloat16),
+        out_specs=ANY,
+        out_shape=jax.ShapeDtypeStruct(shape, jnp.bfloat16),
+        scratch_shapes=[pltpu.VMEM(shape, jnp.bfloat16), pltpu.SemaphoreType.DMA((lists // 4,))],
         compiler_params=SMALL,
         name="pick_near",
     )(left, right, slots)

time: 90.1 us -> 89.9 us (level)
  no operation moved by 1% of the time
where the time goes in v6:
time: 89.9 us; the launch traced here: 89.5 us
  blocking collectives  39.4 us (44%)
  waiting for transfers between devices  21.4 us (24%)
  Pallas kernels  19.9 us (22%)
  starting transfers between devices  8.63 us (10%)
    all_to_all x2, blocking collectives, exchange(): lax.all_to_all(outgoing, axes, split_axis=0, concat_axis=0, tiled=True)  39.4 us
    ppermute x2, waiting for transfers between devices, mirror(): return lax.ppermute(block, 'hi', [(0, 1), (1, 0)])  21.4 us
    pallas_call x1, Pallas kernels, aggregate_inner(): pl.pallas_call(functools.partial(inner_kernel, groups=groups), in_specs=[...  8.2 us
    all_to_all x1, starting transfers between devices, exchange(): lax.all_to_all(outgoing, axes, split_axis=0, concat_axis=0, tiled=True)  6.25 us
    pallas_call x1, Pallas kernels, aggregate_outer(): pl.pallas_call(outer_kernel, in_specs=[SMEM, ANY, ANY, HBM, VMEM, VMEM],...  5.67 us
    ppermute x2, starting transfers between devices, mirror(): return lax.ppermute(block, 'hi', [(0, 1), (1, 0)])  2.38 us
    pallas_call x1, Pallas kernels, project(): pl.pallas_call(functools.partial(project_kernel, groups=groups), in_specs...  2.08 us
    pallas_call x1, Pallas kernels, pick_near(): pl.pallas_call(pick_near_kernel, in_specs=[VMEM, VMEM, VMEM], out_specs=A...  2.04 us
  transfers between devices with their start and end apart: 3, of which 1 were waited for; matrix products, arithmetic and copies ran while one was open for 0% of the time, Pallas kernels for 2%

profile of v6, /device:TPU:1, one launch (start us, length us, event | category | flops | bytes accessed | tf_op | source)
XLA Modules:
  0.0 89.5 jit_solution(12141862119749247535)
XLA Ops:
  0.0 2.1 %project.1 = (bf16[400,256]{1,0:T(8,128)(2,1)S(1)}, bf16[640,256]{1,0:T(8,128)(2,1)S(1)}, s32[128,16]{1,0:T(8,128)S(1)}) custom-call(s32[1]{0:T(128)} %bitcast.side_ref, bf16[602,1024]{1,0:T(8,128)(2,1)} %bitcast.8, bf16[602,256]{1,0:T(8,128)(2,1)} %w_ref.1, s32[8,128]{1,0:T(8,128)} %bitcast.11, s32[32,128]{1,0:T(8,128)} %bitcast.9), custom_call_target="tpu_custom_call" | custom-call | tf_op jit(solution)/shard_map/project/pallas_call | solution.py:77
  2.1 0.0 copy-start
  2.1 0.0 copy-start.1
  2.1 2.0 %pick_near.1 = bf16[16,128,256]{2,1,0:T(8,128)(2,1)} custom-call(bf16[400,256]{1,0:T(8,128)(2,1)S(1)} %get-tuple-element.12.left_ref.left, bf16[640,256]{1,0:T(8,128)(2,1)S(1)} %get-tuple-element.13.right_ref.right, s32[128,16]{1,0:T(8,128)S(1)} %get-tuple-element.14.slots_ref), custom_call_target="tpu_custom_call" | custom-call | tf_op jit(solution)/shard_map/pick_near/pallas_call | solution.py:116
  4.2 6.2 %all-to-all-start = ((bf16[16,128,256]{2,1,0:T(8,128)(2,1)}), bf16[16,128,256]{2,1,0:T(8,128)(2,1)S(1)}, u32[]{:S(2)}, u32[]{:S(2)}) async-start(bf16[16,128,256]{2,1,0:T(8,128)(2,1)} %pick_near.1), calls=%async_computation | async-start | bytes 2097152 | tf_op jit(solution)/shard_map/all_to_all | solution.py:357
  10.4 2.3 %collective-permute-start.1 = (bf16[640,256]{1,0:T(8,128)(2,1)S(1)}, bf16[640,256]{1,0:T(8,128)(2,1)S(1)}, u32[]{:S(2)}, u32[]{:S(2)}) collective-permute-start(bf16[640,256]{1,0:T(8,128)(2,1)S(1)} %get-tuple-element.13.right_ref.right), channel_id=1, source_target_pairs={{0,2},{2,0},{1,3},{3,1},{4,6},{6,4},{5,7},{7,5},{8,10},{10,8},{9,1... | collective-permute-start | bytes 983048 | tf_op jit(solution)/shard_map/ppermute | solution.py:361
  12.7 0.1 collective-permute-start
  12.8 21.4 %collective-permute-done.left_ref = bf16[400,256]{1,0:T(8,128)(2,1)S(1)} collective-permute-done((bf16[400,256]{1,0:T(8,128)(2,1)S(1)}, bf16[400,256]{1,0:T(8,128)(2,1)S(1)}, u32[]{:S(2)}, u32[]{:S(2)}) %collective-permute-start) | collective-permute-done | bytes 204832 | tf_op jit(solution)/shard_map/ppermute | solution.py:361
  34.2 0.9 pick_left.1
  35.1 0.0 collective-permute-done.1.right_ref
  35.1 1.1 %pick_right.1 = bf16[16,128,256]{2,1,0:T(8,128)(2,1)S(1)} custom-call(bf16[16,128,256]{2,1,0:T(8,128)(2,1)S(1)} %get-tuple-element.15.part_ref, s32[128,16]{1,0:T(8,128)S(1)} %get-tuple-element.16.slots_ref, bf16[640,256]{1,0:T(8,128)(2,1)S(1)} %collective-permute-done.1.right_ref), custom_call_target="tpu_custom_call" | custom-call | tf_op jit(solution)/shard_map/pick_right/pallas_call | solution.py:160
  36.2 0.0 all-to-all-done.near
  36.2 0.0 copy-start.3
  36.2 21.9 %all_to_all.15.far = bf16[16,128,256]{2,1,0:T(8,128)(2,1)} all-to-all(bf16[16,128,256]{2,1,0:T(8,128)(2,1)S(1)} %pick_right.1), channel_id=1, replica_groups=mesh['dom'=8,'hi'=2,'lo'=2] {'dom','lo'}, dimensions={0} | all-to-all | bytes 2097152 | tf_op jit(solution)/shard_map/all_to_all | solution.py:357
  58.1 0.0 copy-done
  58.1 0.0 copy-done.1
  58.1 0.0 copy-done.3
  58.1 8.2 %aggregate_inner.1 = (bf16[8,41,128]{2,1,0:T(8,128)(2,1)S(1)}, bf16[32,41,128]{2,1,0:T(8,128)(2,1)S(1)}) custom-call(s32[8,32]{1,0:T(8,128)} %col_ref.3, s32[1]{0:T(128)} %bitcast.side_ref, bf16[400,256]{1,0:T(8,128)(2,1)} %copy-done.1, bf16[640,256]{1,0:T(8,128)(2,1)} %copy-done, bf16[16,128,256]{2,1,0:T(8,128)(2,1)} %copy-done.3, ...), custom_call_target="tpu_custom_call" | custom-call | tf_op jit(solution)/shard_map/aggregate_inner/pallas_call | solution.py:277
  66.3 0.0 copy-start.2
  66.4 17.5 %all_to_all.16.arrived = bf16[32,41,128]{2,1,0:T(8,128)(2,1)} all-to-all(bf16[32,41,128]{2,1,0:T(8,128)(2,1)S(1)} %get-tuple-element.18), channel_id=1, replica_groups=mesh['dom'=8,'hi'=2,'lo'=2] {'dom','hi','lo'}, dimensions={0} | all-to-all | bytes 671744 | tf_op jit(solution)/shard_map/all_to_all | solution.py:357
  83.8 0.0 copy-done.2
  83.8 5.7 %aggregate_outer.1 = f32[41,1024]{1,0:T(8,128)} custom-call(s32[8,32]{1,0:T(8,128)} %col_ref.3, bf16[8,41,128]{2,1,0:T(8,128)(2,1)} %copy-done.2, bf16[32,41,128]{2,1,0:T(8,128)(2,1)} %all_to_all.16.arrived, bf16[8,32,128,128]{3,2,1,0:T(8,128)(2,1)} %tiles.3, s32[8,128]{1,0:T(8,128)} %bitcast.13, f32[1,41]{1,0:T(1,128)} %bitcast.16), custom_call_target="tpu_custom_call" | custom-call | tf_op jit(solution)/shard_map/aggregate_outer/pallas_call | solution.py:341
Async XLA Ops:
  2.1 56.0 %copy-start = (bf16[640,256]{1,0:T(8,128)(2,1)}, bf16[640,256]{1,0:T(8,128)(2,1)S(1)}, u32[]{:S(2)}) copy-start(bf16[640,256]{1,0:T(8,128)(2,1)S(1)} %get-tuple-element.13.right_ref.right) | copy-start | bytes 983044
  2.1 56.0 %copy-start.1 = (bf16[400,256]{1,0:T(8,128)(2,1)}, bf16[400,256]{1,0:T(8,128)(2,1)S(1)}, u32[]{:S(2)}) copy-start(bf16[400,256]{1,0:T(8,128)(2,1)S(1)} %get-tuple-element.12.left_ref.left) | copy-start | bytes 614404
  4.2 32.0 %all-to-all-start = ((bf16[16,128,256]{2,1,0:T(8,128)(2,1)}), bf16[16,128,256]{2,1,0:T(8,128)(2,1)S(1)}, u32[]{:S(2)}, u32[]{:S(2)}) async-start(bf16[16,128,256]{2,1,0:T(8,128)(2,1)} %pick_near.1), calls=%async_computation | async-start | bytes 2097152 | tf_op jit(solution)/shard_map/all_to_all | solution.py:357
  10.4 24.7 %collective-permute-start.1 = (bf16[640,256]{1,0:T(8,128)(2,1)S(1)}, bf16[640,256]{1,0:T(8,128)(2,1)S(1)}, u32[]{:S(2)}, u32[]{:S(2)}) collective-permute-start(bf16[640,256]{1,0:T(8,128)(2,1)S(1)} %get-tuple-element.13.right_ref.right), channel_id=1, source_target_pairs={{0,2},{2,0},{1,3},{3,1},{4,6},{6,4},{5,7},{7,5},{8,10},{10,8},{9,1... | collective-permute-start | bytes 983048 | tf_op jit(solution)/shard_map/ppermute | solution.py:361
  12.7 21.5 %collective-permute-start = (bf16[400,256]{1,0:T(8,128)(2,1)S(1)}, bf16[400,256]{1,0:T(8,128)(2,1)S(1)}, u32[]{:S(2)}, u32[]{:S(2)}) collective-permute-start(bf16[400,256]{1,0:T(8,128)(2,1)S(1)} %get-tuple-element.12.left_ref.left), channel_id=1, source_target_pairs={{0,2},{2,0},{1,3},{3,1},{4,6},{6,4},{5,7},{7,5},{8,10},{10,8},{9,1... | collective-permute-start | bytes 614408 | tf_op jit(solution)/shard_map/ppermute | solution.py:361
  36.2 21.9 %copy-start.3 = (bf16[16,128,256]{2,1,0:T(8,128)(2,1)}, bf16[16,128,256]{2,1,0:T(8,128)(2,1)S(1)}, u32[]{:S(2)}) copy-start(bf16[16,128,256]{2,1,0:T(8,128)(2,1)S(1)} %all-to-all-done.near) | copy-start | bytes 3145732
  66.3 17.5 %copy-start.2 = (bf16[8,41,128]{2,1,0:T(8,128)(2,1)}, bf16[8,41,128]{2,1,0:T(8,128)(2,1)S(1)}, u32[]{:S(2)}) copy-start(bf16[8,41,128]{2,1,0:T(8,128)(2,1)S(1)} %get-tuple-element.17.own) | copy-start | bytes 251908
